TPU v7x, 128 devices: a whole 4x4x4 slice. The times are simulated.
128 devices in a mesh: view: 8 (over z, core), tile: 16 (over x, y).
Axes of the slice: x: 4, y: 4, z: 4, core: 2. Of those that a mesh axis runs over, the one named last changes fastest.
Arguments:
- sdf_value: float32 [24576, 256], P(('view', 'tile')), may hold values from -1 to 1
- weight: float32 [24576, 256], P(('view', 'tile')), may hold values from 0.25 to 4
- color: float32 [3, 24576, 256], P(None, ('view', 'tile')), may hold values from 0 to 1
- voxel_index: int32 [24576, 256], P(('view', 'tile')), may hold values from 0 to 511
- valid: int32 [24576, 256], P(('view', 'tile')), may hold values 0 or 1
- list_count: int32 [24576], P(('view', 'tile')), may hold values from 1 to 256
- list_key: int32 [24576], P(('view', 'tile')), may hold values from 0 to 8191, as said below
- owner_slot: int32 [8192], replicated, may hold values from 0 to 8191, as said below
Outputs:
- joined_tsdf: float32 [8192, 512], P(('view', 'tile'))
- joined_color: float32 [8192, 3, 512], P(('view', 'tile'))
- block_counts: int32 [8192], replicated
Inputs may be any that keep to these rules, and one draw needn't show every extreme that they name: `owner_slot`: each block key has one storage row and each row one key. Of the 192 lists of one device, at most 6 have a storage row owner_slot[list_key] among the 64 rows of any one device; some device receives exactly 6 lists from every device.
All inputs are finite; a program needn't handle non-finite values. No bound on the sum of `valid` on one device may be relied on, other than what follows from the above.
Results may differ from a plain program's by a relative error of at most 0.0037.
Values may be sent and summed in bfloat16 or wider, within the bound.
No kernel may reach another device: no remote copies, remote signals or barrier semaphores. Data moves between devices by JAX's collectives and lax.ppermute only.
A program may use at most 64 MiB of HBM per device.

v0:
```python
import jax
import jax.numpy as jnp
from jax import lax
from jax.sharding import Mesh
from jax.sharding import PartitionSpec as P

VOX = 512
VIEW_TILE = ("view_0", "view_1", "tile_0", "tile_1")


def joined_along(parts, dim):
    dims = list(parts.shape[1:])
    dims[dim] *= parts.shape[0]
    return jnp.moveaxis(parts, 0, dim).reshape(dims)


def stacked_from(shard, axes, order):
    parts = shard[None]
    for k in order:
        parts = lax.all_gather(parts, axes[k], axis=0, tiled=True)
    held = [lax.axis_size(axes[k]) for k in reversed(order)]
    parts = parts.reshape(*held, *shard.shape)
    turned = sorted(range(len(order)), key=lambda place: order[len(order) - 1 - place])
    return parts.transpose(*turned, *range(len(order), parts.ndim)).reshape(-1, *shard.shape)


def whole_of(shard, axes, order, dim):
    return joined_along(stacked_from(shard, axes, order), dim)


def deliver(parcels):
    return (
        lax.all_to_all(
            parcels[0].astype(jnp.bfloat16), VIEW_TILE, split_axis=0, concat_axis=0, tiled=True
        ).astype(jnp.float32),
        lax.all_to_all(parcels[1], VIEW_TILE, split_axis=0, concat_axis=0, tiled=True),
    )


def on_device(sdf_value, weight, color, voxel_index, valid, list_count, list_key, owner_slot):
    list_rows, points = sdf_value.shape
    devices = lax.axis_size(VIEW_TILE)
    blocks_all = owner_slot.shape[0]
    blocks_dev = blocks_all // devices
    block_capacity = 4 * list_rows // devices
    total_slots = devices * block_capacity
    position = jnp.arange(points, dtype=jnp.int32)
    live_mask = ((position[None, :] < list_count[:, None]) & (valid == 1)).astype(jnp.float32)
    scaled = live_mask * weight
    payload = jnp.stack(
        [
            live_mask,
            scaled,
            scaled * sdf_value,
            scaled * color[0],
            scaled * color[1],
            scaled * color[2],
        ],
        axis=1,
    ).astype(jnp.bfloat16)
    key_match = list_key[:, None] == jnp.arange(blocks_all, dtype=jnp.int32)[None, :]
    storage = jnp.sum(jnp.where(key_match, owner_slot[None, :], 0), axis=1)
    owner_dev = storage // blocks_dev
    block_row = storage % blocks_dev
    owner_hot = (owner_dev[:, None] == jnp.arange(devices, dtype=jnp.int32)[None, :]).astype(
        jnp.int32
    )
    arrival_order = jnp.sum(jnp.cumsum(owner_hot, axis=0) * owner_hot, axis=1) - 1
    slot_index = owner_dev * block_capacity + arrival_order
    placement = slot_index[None, :] == jnp.arange(total_slots, dtype=jnp.int32)[:, None]
    send_rows = jnp.full((total_slots,), -1, jnp.int32).at[slot_index].set(block_row)
    block_ids = jnp.arange(blocks_dev, dtype=jnp.int32)
    voxel_ids = jnp.arange(VOX, dtype=jnp.int32)
    voxel_onehot = (voxel_index[:, :, None] == voxel_ids[None, None, :]).astype(jnp.bfloat16)
    partial_value = jnp.einsum(
        "lcp,lpv->lcv", payload, voxel_onehot, preferred_element_type=jnp.float32
    )
    send_parts = jnp.dot(
        placement.astype(jnp.float32),
        partial_value.reshape(list_rows, -1),
        precision=lax.Precision.HIGHEST,
        preferred_element_type=jnp.float32,
    )
    got_parts, got_rows = deliver((send_parts, send_rows))
    row_hot = (got_rows[:, None] == block_ids[None, :]).astype(jnp.float32)
    voxel_sums = jnp.einsum(
        "gb,gk->bk",
        row_hot,
        got_parts,
        precision=lax.Precision.HIGHEST,
        preferred_element_type=jnp.float32,
    )
    voxel_sums = voxel_sums.reshape(blocks_dev, 6, VOX)
    local_counts = jnp.sum(voxel_sums[:, 0, :], axis=1).astype(jnp.int32)
    block_counts = whole_of(local_counts, VIEW_TILE, (0, 2, 3, 1), 0)
    divisor = jnp.maximum(voxel_sums[:, 1, :], 1.0)
    joined_tsdf = voxel_sums[:, 2, :] / divisor
    joined_color = voxel_sums[:, 3:6, :] / divisor[:, None, :]
    return (joined_tsdf, joined_color, block_counts)


def solution(mesh):
    finer = Mesh(mesh.devices.reshape(4, 2, 4, 4), ("view_0", "view_1", "tile_0", "tile_1"))
    placed = (
        P(VIEW_TILE, None),
        P(VIEW_TILE, None),
        P(None, VIEW_TILE, None),
        P(VIEW_TILE, None),
        P(VIEW_TILE, None),
        P(VIEW_TILE),
        P(VIEW_TILE),
        P(),
    )
    return jax.shard_map(
        on_device,
        mesh=finer,
        in_specs=placed,
        out_specs=(P(VIEW_TILE, None), P(VIEW_TILE, None, None), P()),
        check_vma=False,
    )
```

profile of v0, /device:TPU:1, one launch (start us, length us, event | category | flops | bytes accessed | tf_op | source)
XLA Modules:
  0.0 200.0 jit_solution(10806507833486373694)
XLA Ops:
  0.6 0.0 copy-start
  0.6 1.8 select_reduce_fusion
  2.4 0.1 iota_compare_fusion.7
  2.6 0.1 fusion.11
  2.8 0.2 fusion.19
  3.0 1.2 scatter_custom_fusion
  4.2 0.8 all_to_all.14
  5.0 11.5 %all-to-all-start = ((s32[128,6,1]{1,2,0:T(1,128)}), s32[128,6,1]{1,2,0:T(1,128)S(1)}, u32[]{:S(2)}, u32[]{:S(2)}) async-start(s32[128,6,1]{1,2,0:T(1,128)} %bitcast.7), calls=%async_computation | async-start | bytes 131072 | tf_op jit(solution)/shard_map/all_to_all | solution.py:36
  16.5 1.2 fusion.18
  17.7 1.0 convert_bitcast_fusion
  18.7 1.3 fusion.17
  20.0 0.2 copy.87
  20.2 0.2 copy.88
  20.3 0.2 copy.89
  20.5 0.2 copy.85
  20.6 0.2 copy.86
  20.8 0.2 copy.90
  21.0 1.8 stack.37
  22.8 0.0 copy-done
  22.8 23.8 %fusion = f32[192,6,512]{2,1,0:T(8,128)S(1)} fusion(bf16[192,6,256]{2,1,0:T(8,128)(2,1)S(1)} %stack.37, s32[192,256]{1,0:T(8,128)S(1)} %copy-done), kind=kOutput, calls=%fused_computation.2 | convolution fusion | flops 327155712 | bytes 3145728 | tf_op jit(solution)/shard_map/lcp,lpv->lcv/dot_general | solution.py:75
  46.6 2.0 %copy.93 = f32[24,8,6,512]{3,1,2,0:T(8,128)S(1)} copy(f32[24,8,6,512]{3,2,1,0:T(8,128)S(1)} %bitcast.67) | data formatting | bytes 4718592
  48.6 5.6 %convolution_convert_fusion = bf16[768,3072]{1,0:T(8,128)(2,1)} fusion(f32[192,3072]{1,0:T(8,128)S(1)} %bitcast.66, s32[192]{0:T(256)S(1)} %get-tuple-element.14), kind=kOutput, calls=%fused_computation.6 | convolution fusion | flops 5438324736 | bytes 7078656 | tf_op jit(solution)/shard_map/dot_general | solution.py:78
  54.2 7.7 %all_to_all.16 = bf16[128,6,3072]{2,1,0:T(8,128)(2,1)} reshape(bf16[768,3072]{1,0:T(8,128)(2,1)} %convolution_convert_fusion) | data formatting | bytes 9437184 | tf_op jit(solution)/shard_map/all_to_all | solution.py:33
  61.9 0.0 copy-start.1
  61.9 0.0 all-to-all-done
  61.9 10.2 %all-to-all-start.1 = ((bf16[128,6,3072]{2,1,0:T(8,128)(2,1)}), bf16[128,6,3072]{2,1,0:T(8,128)(2,1)}, u32[]{:S(2)}, u32[]{:S(2)}) async-start(bf16[128,6,3072]{2,1,0:T(8,128)(2,1)} %all_to_all.16), calls=%async_computation.1 | async-start | bytes 12582912 | tf_op jit(solution)/shard_map/all_to_all | solution.py:33
  72.1 0.0 copy-done.1
  72.1 0.6 dynamic-slice
  73.3 0.5 broadcast.215
  73.8 0.8 reduce.4
  74.6 0.1 eq.91
  74.8 72.7 %all-to-all-done.1 = bf16[128,6,3072]{2,1,0:T(8,128)(2,1)} async-done(((bf16[128,6,3072]{2,1,0:T(8,128)(2,1)}), bf16[128,6,3072]{2,1,0:T(8,128)(2,1)}, u32[]{:S(2)}, u32[]{:S(2)}) %all-to-all-start.1) | async-done | bytes 4718624 | tf_op jit(solution)/shard_map/all_to_all | solution.py:33
  147.5 7.8 %all_to_all.18 = bf16[768,3072]{1,0:T(8,128)(2,1)} reshape(bf16[128,6,3072]{2,1,0:T(8,128)(2,1)} %all-to-all-done.1) | data formatting | bytes 9437184 | tf_op jit(solution)/shard_map/all_to_all | solution.py:33
  155.3 6.6 %copy.91 = bf16[3072,768]{1,0:T(8,128)(2,1)} copy(bf16[3072,768]{0,1:T(8,128)(2,1)} %bitcast.65) | data formatting | bytes 9437184 | tf_op jit(solution)/shard_map/gb,gk->bk/dot_general | solution.py:86
  161.9 3.9 %fusion.7 = f32[64,6,512]{2,0,1:T(8,128)S(1)} fusion(bf16[6,512,768]{2,1,0:T(8,128)(2,1)} %bitcast.64, s32[768]{0:T(1024)S(1)} %eq.91), kind=kOutput, calls=%fused_computation.21 | convolution fusion | flops 302039040 | bytes 5508096 | tf_op jit(solution)/shard_map/gb,gk->bk/dot_general | solution.py:86
  165.8 0.8 slice_reduce_fusion
  166.6 0.8 slice_divide_fusion
  167.4 0.1 convert_dynamic-update-slice_fusion
  167.5 4.6 %all-reduce.1 = s32[256]{0:T(256)S(1)} all-reduce(s32[256]{0:T(256)S(1)} %convert_dynamic-update-slice_fusion), channel_id=2, replica_groups=mesh['view_0'=4,'view_1'=2,'tile_0'=4,'tile_1'=4] {'view_0'}, use_global_device_ids=true, to_apply=%add.1 | all-reduce | flops 256 | bytes 2048
  172.1 0.1 reshape.162
  172.2 8.2 %all-gather.1 = s32[4,4,64]{2,1,0:T(4,128)S(1)} all-gather(s32[1,4,64]{2,1,0:T(4,128)S(1)} %reshape.162), channel_id=1, replica_groups=mesh['view_0'=4,'view_1'=2,'tile_0'=4,'tile_1'=4] {'tile_0'}, dimensions={0}, use_global_device_ids=true | all-gather | bytes 5120 | tf_op jit(solution)/shard_map/all_gather | solution.py:20
  180.3 9.0 %all_gather.14 = s32[64,64]{1,0:T(8,128)S(1)} all-gather(s32[16,64]{1,0:T(8,128)S(1)} %bitcast.73), channel_id=1, replica_groups=mesh['view_0'=4,'view_1'=2,'tile_0'=4,'tile_1'=4] {'tile_1'}, dimensions={0}, use_global_device_ids=true | all-gather | bytes 20480 | tf_op jit(solution)/shard_map/all_gather | solution.py:20
  189.4 9.9 %all_gather.15 = s32[128,64]{1,0:T(8,128)S(1)} all-gather(s32[64,64]{1,0:T(8,128)S(1)} %all_gather.14), channel_id=1, replica_groups=mesh['view_0'=4,'view_1'=2,'tile_0'=4,'tile_1'=4] {'view_1'}, dimensions={0}, use_global_device_ids=true | all-gather | bytes 49152 | tf_op jit(solution)/shard_map/all_gather | solution.py:20
  199.3 0.7 reshape_reshape.3
  (13 shorter events, 0.2 us)
Async XLA Ops:
  0.6 22.2 %copy-start = (s32[192,256]{1,0:T(8,128)S(1)}, s32[192,256]{1,0:T(8,128)}, u32[]{:S(2)}) copy-start(s32[192,256]{1,0:T(8,128)} %param.11) | copy-start | bytes 589828
  5.0 56.9 %all-to-all-start = ((s32[128,6,1]{1,2,0:T(1,128)}), s32[128,6,1]{1,2,0:T(1,128)S(1)}, u32[]{:S(2)}, u32[]{:S(2)}) async-start(s32[128,6,1]{1,2,0:T(1,128)} %bitcast.7), calls=%async_computation | async-start | bytes 131072 | tf_op jit(solution)/shard_map/all_to_all | solution.py:36
  61.9 10.2 %copy-start.1 = (u32[128]{0:T(128)S(1)}, u32[128]{0:T(128)}, u32[]{:S(2)}) copy-start(u32[128]{0:T(128)} %constant.59) | copy-start | bytes 1540
  61.9 85.6 %all-to-all-start.1 = ((bf16[128,6,3072]{2,1,0:T(8,128)(2,1)}), bf16[128,6,3072]{2,1,0:T(8,128)(2,1)}, u32[]{:S(2)}, u32[]{:S(2)}) async-start(bf16[128,6,3072]{2,1,0:T(8,128)(2,1)} %all_to_all.16), calls=%async_computation.1 | async-start | bytes 12582912 | tf_op jit(solution)/shard_map/all_to_all | solution.py:33
where the time goes:
time: 201 us; the launch traced here: 200 us
  waiting for transfers between devices  72.7 us (36%)
  matrix products  33.3 us (17%)
  blocking collectives  31.7 us (16%)
  local copies, waits for them, and re-layouts  30.9 us (15%)
  starting transfers between devices  21.6 us (11%)
  other arithmetic  8.27 us (4%)
    all_to_all x1, waiting for transfers between devices, deliver(): lax.all_to_all(parcels[0].astype(jnp.bfloat16), VIEW_TILE, split_axis=0,...  72.7 us
    all_gather x3, blocking collectives, stacked_from(): parts = lax.all_gather(parts, axes[k], axis=0, tiled=True)  27.1 us
    dot_general x1, matrix products, on_device(): jnp.einsum('lcp,lpv->lcv', payload, voxel_onehot, preferred_element_type=...  23.8 us
    all_to_all x2, local copies, waits for them, and re-layouts, deliver(): lax.all_to_all(parcels[0].astype(jnp.bfloat16), VIEW_TILE, split_axis=0,...  15.5 us
    all_to_all x1, starting transfers between devices, deliver(): lax.all_to_all(parcels[1], VIEW_TILE, split_axis=0, concat_axis=0, tiled=...  11.5 us
    all_to_all x1, starting transfers between devices, deliver(): lax.all_to_all(parcels[0].astype(jnp.bfloat16), VIEW_TILE, split_axis=0,...  10.2 us
    dot_general x1, local copies, waits for them, and re-layouts, on_device(): jnp.einsum('gb,gk->bk', row_hot, got_parts, precision=lax.Precision.HIGHE...  6.62 us
    dot_general x1, matrix products, on_device(): jnp.dot(placement.astype(jnp.float32), partial_value.reshape(list_rows, -...  5.62 us
  transfers between devices with their start and end apart: 2, of which 1 were waited for; matrix products, arithmetic and copies ran while one was open for 20% of the time, Pallas kernels for 0%

commit v1 on v0

v1 whole, which is shorter than its diff:
```python
import jax
import jax.numpy as jnp
from jax import lax
from jax.experimental import pallas as pl
from jax.experimental.pallas import tpu as pltpu
from jax.sharding import PartitionSpec as P

AXES = ("view", "tile")
DEVICES = 128
LISTS = 192
PTS = 256
BLOCKS = 64
CAP = 6
VALUES = 6
ROWS = CAP * VALUES * 2
HIGH = 8
LOW = 64
STRIDE = 72
META = 256
STEP = 16
F32 = jnp.float32
BF16 = jnp.bfloat16
I32 = jnp.int32
VMEM = pl.BlockSpec(memory_space=pltpu.VMEM)
NT = (((1,), (1,)), ((), ()))


def iota(shape, dim):
    return lax.broadcasted_iota(I32, shape, dim)


def hot(cond):
    return jnp.where(cond, 1.0, 0.0).astype(BF16)


def dot(a, b):
    return jnp.dot(a, b, preferred_element_type=F32)


def pack_kernel(sdf, weight, color, voxel, valid, count, key, table, send, meta, x, rows):
    key_row = key[...]
    high_hot = hot((key_row >> 7) == iota((64, LISTS), 0))
    low_hot = jnp.where((key_row & 127) == iota((128, LISTS), 0), 1.0, 0.0)
    slots = table[...]
    owner_of = (slots >> 6).astype(F32).T.astype(BF16)
    row_of = (slots & 63).astype(F32).T.astype(BF16)
    owner = jnp.sum(dot(owner_of, high_hot) * low_hot, axis=0, keepdims=True)
    row = jnp.sum(dot(row_of, high_hot) * low_hot, axis=0, keepdims=True)
    owner_hot = jnp.where(owner.astype(I32) == iota((DEVICES, LISTS), 0), 1.0, 0.0)
    before = hot(iota((LISTS, LISTS), 0) < iota((LISTS, LISTS), 1))
    order = jnp.sum(dot(owner_hot.astype(BF16), before) * owner_hot, axis=0, keepdims=True)

    diagonal = iota((LISTS, LISTS), 0) == iota((LISTS, LISTS), 1)
    spread = jnp.where(diagonal, count[...].astype(F32), 0.0).astype(BF16)
    used = dot(spread, jnp.ones((LISTS, PTS), BF16))
    live = (iota((LISTS, PTS), 1).astype(F32) < used) & (valid[...] == 1)
    mask = jnp.where(live, 1.0, 0.0)
    live_count = lax.dot_general(
        jnp.ones((8, PTS), BF16), mask.astype(BF16), NT, preferred_element_type=F32
    )[0:1]
    packed = (owner.astype(I32) * 64 + row.astype(I32)) * 512 + live_count.astype(I32)
    meta[...] = jnp.concatenate([packed, jnp.zeros((1, META - LISTS), I32)], axis=1)

    scaled = mask * weight[...]
    values = [
        (voxel[...] - 256).astype(F32),
        scaled,
        scaled * sdf[...],
        scaled * color[0],
        scaled * color[1],
        scaled * color[2],
    ]
    for v, value in enumerate(values):
        value = value.astype(BF16)
        for half in range(2):
            j = half * VALUES + v
            x[:, j * 128 : (j + 1) * 128] = value[:, half * 128 : (half + 1) * 128]

    for k in range(CAP):
        place = jnp.where(order == k, owner_hot, 0.0).astype(BF16)
        for j in range(0, 2 * VALUES, 2):
            moved = dot(place, x[:, j * 128 : (j + 2) * 128])
            for side in range(2):
                at = k * 2 * VALUES + j + side
                rows[pl.ds(at, DEVICES, stride=STRIDE), :] = moved[
                    :, side * 128 : (side + 1) * 128
                ]

    def convert(i, carry):
        at = pl.multiple_of(i * 144, 144)
        send[pl.ds(at, 144), :] = rows[pl.ds(at, 144), :].astype(BF16)
        return carry

    lax.fori_loop(0, DEVICES // 2, convert, 0)


def count_kernel(gathered, counts, heads):
    me = lax.axis_index("view") * 16 + lax.axis_index("tile")

    def body(s, total):
        line = gathered[pl.ds(s, 1), :]
        storage = line >> 9
        number = (line & 511).astype(F32)
        a = jnp.where((storage >> 7) == iota((64, META), 0), number, 0.0).astype(BF16)
        b = hot((storage & 127) == iota((128, META), 0))
        return total + lax.dot_general(a, b, NT, preferred_element_type=F32)

    counts[...] = lax.fori_loop(
        0, DEVICES, body, jnp.zeros((64, 128), F32), unroll=4
    ).astype(I32)

    turned = gathered[...].T
    mine = ((turned >> 15) == me) & (iota((META, DEVICES), 0) < LISTS)
    row = ((turned >> 9) & 63) + 1
    before = hot(iota((META, META), 1) < iota((META, META), 0))
    order = dot(before, hot(mine)).astype(I32)
    lines = []
    for k in range(CAP):
        at = jnp.sum(jnp.where(mine & (order == k), row, 0), axis=0, keepdims=True)
        lines.append(jnp.where(at == 0, BLOCKS, at - 1))
    lines.append(jnp.full((2, DEVICES), BLOCKS, I32))
    heads[...] = jnp.concatenate(lines, axis=0)


def join_kernel(heads, got, tsdf, color, total, work):
    step = pl.program_id(0)

    @pl.when(step == 0)
    def _():
        total[...] = jnp.zeros_like(total)
        work[...] = jnp.zeros_like(work)

    low_id = iota((LOW, 128), 0).astype(F32)

    def body(i, carry):
        work[0:ROWS, :] = got[i].astype(F32)
        for k in range(CAP):
            a_parts, b_parts = [], []
            for half in range(2):
                at = (2 * k + half) * VALUES
                index = jnp.broadcast_to(work[at : at + 1, :], (8, 128))
                high = jnp.floor(index * (1.0 / LOW))
                low = index - high * LOW
                low_all = jnp.concatenate([low] * (LOW // 8), axis=0)
                b_parts.append(jnp.where(low_all == low_id, 1.0, 0.0))
                group = work[at : at + 8, :]
                a_parts.append(
                    jnp.concatenate(
                        [jnp.where(high == float(h - 4), group, 0.0) for h in range(HIGH)],
                        axis=0,
                    )
                )
            a = jnp.concatenate(a_parts, axis=1).astype(BF16)
            b = jnp.concatenate(b_parts, axis=1).astype(BF16)
            part = lax.dot_general(a, b, NT, preferred_element_type=F32)
            where = pl.ds(pl.multiple_of(heads[k, step * STEP + i] * STRIDE, 8), HIGH * 8)
            total[where, 0:LOW] += part
        return carry

    lax.fori_loop(0, STEP, body, 0)

    @pl.when(step == DEVICES // STEP - 1)
    def _():
        for h in range(HIGH):

            def channel(c):
                return total[pl.ds(h * 8 + c, BLOCKS, stride=STRIDE), :][:, 0:LOW]

            span = slice(h * LOW, (h + 1) * LOW)
            divisor = jnp.maximum(channel(1), 1.0)
            tsdf[:, span] = channel(2) / divisor
            for c in range(3):
                color[c, :, span] = channel(3 + c) / divisor


def on_device(sdf_value, weight, color, voxel_index, valid, list_count, list_key, owner_slot):
    send, meta = pl.pallas_call(
        pack_kernel,
        out_shape=(
            jax.ShapeDtypeStruct((DEVICES * ROWS, 128), BF16),
            jax.ShapeDtypeStruct((1, META), I32),
        ),
        in_specs=[VMEM] * 8,
        out_specs=(VMEM, VMEM),
        scratch_shapes=[
            pltpu.VMEM((LISTS, 2 * VALUES * 128), BF16),
            pltpu.VMEM((DEVICES * STRIDE, 128), F32),
        ],
        name="pack",
    )(
        sdf_value,
        weight,
        color,
        voxel_index,
        valid,
        list_count.reshape(1, LISTS),
        list_key.reshape(1, LISTS),
        owner_slot.reshape(64, 128),
    )
    got = lax.all_to_all(
        send.reshape(DEVICES, ROWS, 128), AXES, split_axis=0, concat_axis=0, tiled=True
    )
    gathered = lax.all_gather(meta, AXES, axis=0, tiled=True)
    counts, heads = pl.pallas_call(
        count_kernel,
        out_shape=(
            jax.ShapeDtypeStruct((64, 128), I32),
            jax.ShapeDtypeStruct((8, DEVICES), I32),
        ),
        in_specs=[VMEM],
        out_specs=(VMEM, VMEM),
        cost_estimate=pl.CostEstimate(flops=400_000_000, bytes_accessed=200_000, transcendentals=0),
        name="count",
    )(gathered)
    tsdf, colors = pl.pallas_call(
        join_kernel,
        grid=(DEVICES // STEP,),
        out_shape=(
            jax.ShapeDtypeStruct((BLOCKS, 512), F32),
            jax.ShapeDtypeStruct((3, BLOCKS, 512), F32),
        ),
        in_specs=[
            pl.BlockSpec(memory_space=pltpu.SMEM),
            pl.BlockSpec((STEP, ROWS, 128), lambda g: (g, 0, 0)),
        ],
        out_specs=(
            pl.BlockSpec((BLOCKS, 512), lambda g: (0, 0)),
            pl.BlockSpec((3, BLOCKS, 512), lambda g: (0, 0, 0)),
        ),
        scratch_shapes=[
            pltpu.VMEM(((BLOCKS + 1) * STRIDE, 128), F32),
            pltpu.VMEM((80, 128), F32),
        ],
        name="join",
    )(heads, got)
    return tsdf, jnp.transpose(colors, (1, 0, 2)), counts.reshape(DEVICES * BLOCKS)


def solution(mesh):
    return jax.shard_map(
        on_device,
        mesh=mesh,
        in_specs=(
            P(AXES, None),
            P(AXES, None),
            P(None, AXES, None),
            P(AXES, None),
            P(AXES, None),
            P(AXES),
            P(AXES),
            P(),
        ),
        out_specs=(P(AXES, None), P(AXES, None, None), P()),
        check_vma=False,
    )
```

time: 201 us -> 135 us (0.67)
  waiting for transfers between devices: 72.7 us -> 0.01 us
  Pallas kernels: 0 us -> 45 us
  blocking collectives: 31.7 us -> 75.9 us
  matrix products: 33.3 us -> 0 us
  local copies, waits for them, and re-layouts: 30.9 us -> 2.08 us
  starting transfers between devices: 21.6 us -> 11.5 us
  other arithmetic: 8.27 us -> 0 us
    all_to_all x2 -> x1, waiting for transfers between devices: 72.7 us -> 0.01 us  [on_device(): lax.all_to_all(send.reshape(DEVICES, ROWS, 128), AXES, split_axis=0, conc...]
    all_gather x3 -> x1, blocking collectives: 27.1 us -> 75.9 us  [on_device(): gathered = lax.all_gather(meta, AXES, axis=0, tiled=True)]
    pallas_call x0 -> x3, Pallas kernels: none -> 45 us  [the longest x1 30.4 us: on_device(): pl.pallas_call(join_kernel, grid=(DEVICES // STEP,), out_shape=(jax.Shape...]
    dot_general x3 -> x0, matrix products: 33.3 us -> none  [the longest x1 23.8 us: on_device(): jnp.einsum('lcp,lpv->lcv', payload, voxel_onehot, preferred_element_type=...]
    all_to_all x4 -> x0, local copies, waits for them, and re-layouts: 16.8 us -> none  [the longest x2 15.5 us: deliver(): lax.all_to_all(parcels[0].astype(jnp.bfloat16), VIEW_TILE, split_axis=0,...]
    all_to_all x2 -> x1, starting transfers between devices: 21.6 us -> 11.5 us  [on_device(): lax.all_to_all(send.reshape(DEVICES, ROWS, 128), AXES, split_axis=0, conc...]
    dot_general x1 -> x0, local copies, waits for them, and re-layouts: 6.62 us -> none  [on_device(): jnp.einsum('gb,gk->bk', row_hot, got_parts, precision=lax.Precision.HIGHE...]
    unnamed x1 -> x0, blocking collectives: 4.61 us -> none
  transfers between devices with their start and end apart: 2 -> 1, of which waited for: 1 -> 0; matrix products, arithmetic and copies ran while one was open for 20% -> 0% of each run, Pallas kernels for 0% -> 7%
where the time goes in v1:
time: 135 us
  blocking collectives  75.9 us (56%)
  Pallas kernels  45 us (33%)
  starting transfers between devices  11.5 us (9%)
  local copies, waits for them, and re-layouts  2.08 us (2%)
    all_gather x1, blocking collectives, on_device(): gathered = lax.all_gather(meta, AXES, axis=0, tiled=True)  75.9 us
    pallas_call x1, Pallas kernels, on_device(): pl.pallas_call(join_kernel, grid=(DEVICES // STEP,), out_shape=(jax.Shape...  30.4 us
    all_to_all x1, starting transfers between devices, on_device(): lax.all_to_all(send.reshape(DEVICES, ROWS, 128), AXES, split_axis=0, conc...  11.5 us
    pallas_call x1, Pallas kernels, on_device(): pl.pallas_call(count_kernel, out_shape=(jax.ShapeDtypeStruct((64, 128), I...  9.54 us
    pallas_call x1, Pallas kernels, on_device(): pl.pallas_call(pack_kernel, out_shape=(jax.ShapeDtypeStruct((DEVICES * RO...  5.02 us
  transfers between devices with their start and end apart: 1, of which 0 were waited for; matrix products, arithmetic and copies ran while one was open for 0% of the time, Pallas kernels for 7%

profile of v1, /device:TPU:1, one launch (start us, length us, event | category | flops | bytes accessed | tf_op | source)
XLA Modules:
  0.0 135.1 jit_solution(15662813301255627606)
XLA Ops:
  0.6 5.0 %pack.1 = (bf16[9216,128]{1,0:T(8,128)(2,1)}, s32[1,256]{1,0:T(1,128)}) custom-call(f32[192,256]{1,0:T(8,128)} %sdf.1, f32[192,256]{1,0:T(8,128)} %weight.1, f32[3,192,256]{2,1,0:T(8,128)} %color.1, s32[192,256]{1,0:T(8,128)} %voxel.1, s32[192,256]{1,0:T(8,128)} %valid.1, s32[1,192]{1,0:T(1,128)} %bitcast.14, s32[1,192]{1,0:T(1,128)} %bitcast.15, ...), custom_call_target="tpu_custom_call" | custom-call | tf_op jit(solution)/shard_map/pack/pallas_call | solution.py:177
  5.7 0.0 copy-start.1
  5.7 11.5 %all-to-all-start = ((bf16[128,72,128]{2,1,0:T(8,128)(2,1)}), bf16[128,72,128]{2,1,0:T(8,128)(2,1)S(1)}, u32[]{:S(2)}, u32[]{:S(2)}) async-start(bf16[128,72,128]{2,1,0:T(8,128)(2,1)} %bitcast.10), calls=%async_computation | async-start | bytes 4718592 | tf_op jit(solution)/shard_map/all_to_all | solution.py:200
  17.2 0.0 copy-done.1
  17.2 75.9 %all-gather = s32[128,1,256]{2,1,0:T(1,128)S(1)} all-gather(s32[1,1,256]{2,1,0:T(1,128)S(1)} %bitcast.13), channel_id=1, replica_groups=mesh['view'=8,'tile'=16] {'view','tile'}, dimensions={0}, use_global_device_ids=true | all-gather | bytes 132096 | tf_op jit(solution)/shard_map/all_gather | solution.py:203
  93.1 0.7 copy.13
  93.7 9.5 %count.1 = (s32[64,128]{1,0:T(8,128)}, s32[8,128]{1,0:T(8,128)}) custom-call(s32[128,256]{1,0:T(8,128)} %bitcast.11), custom_call_target="tpu_custom_call" | custom-call | flops 400000000 | bytes 200000 | tf_op jit(solution)/shard_map/count/pallas_call | solution.py:204
  103.3 0.0 all-to-all-done.got
  103.3 0.0 copy-start
  103.3 1.4 %copy-done = bf16[128,72,128]{2,1,0:T(8,128)(2,1)} copy-done((bf16[128,72,128]{2,1,0:T(8,128)(2,1)}, bf16[128,72,128]{2,1,0:T(8,128)(2,1)S(1)}, u32[]{:S(2)}) %copy-start) | copy-done | bytes 2359320
  104.7 30.4 %join.1 = (f32[64,512]{1,0:T(8,128)}, f32[3,64,512]{2,1,0:T(8,128)}) custom-call(s32[8,128]{1,0:T(8,128)} %get-tuple-element.10.heads, bf16[128,72,128]{2,1,0:T(8,128)(2,1)} %copy-done), custom_call_target="tpu_custom_call" | custom-call | tf_op jit(solution)/shard_map/join/pallas_call | solution.py:215
Async XLA Ops:
  5.7 11.5 %copy-start.1 = (s32[1,256]{1,0:T(1,128)S(1)}, s32[1,256]{1,0:T(1,128)}, u32[]{:S(2)}) copy-start(s32[1,256]{1,0:T(1,128)} %get-tuple-element.9) | copy-start | bytes 3076
  5.7 97.6 %all-to-all-start = ((bf16[128,72,128]{2,1,0:T(8,128)(2,1)}), bf16[128,72,128]{2,1,0:T(8,128)(2,1)S(1)}, u32[]{:S(2)}, u32[]{:S(2)}) async-start(bf16[128,72,128]{2,1,0:T(8,128)(2,1)} %bitcast.10), calls=%async_computation | async-start | bytes 4718592 | tf_op jit(solution)/shard_map/all_to_all | solution.py:200
  103.3 1.4 %copy-start = (bf16[128,72,128]{2,1,0:T(8,128)(2,1)}, bf16[128,72,128]{2,1,0:T(8,128)(2,1)S(1)}, u32[]{:S(2)}) copy-start(bf16[128,72,128]{2,1,0:T(8,128)(2,1)S(1)} %all-to-all-done.got) | copy-start | bytes 7077892

commit v2 on v1

v2 whole, which is shorter than its diff:
```python
import jax
import jax.numpy as jnp
from jax import lax
from jax.experimental import pallas as pl
from jax.experimental.pallas import tpu as pltpu
from jax.sharding import PartitionSpec as P

AXES = ("view", "tile")
DEVICES = 128
LISTS = 192
PTS = 256
BLOCKS = 64
CAP = 6
VALUES = 6
DATA = CAP * VALUES * 2
ROWS = DATA + 8
HIGH = 8
LOW = 64
STRIDE = 72
META = 256
SOURCES = 2
WORK = 80
F32 = jnp.float32
BF16 = jnp.bfloat16
I32 = jnp.int32
VMEM = pl.BlockSpec(memory_space=pltpu.VMEM)
NT = (((1,), (1,)), ((), ()))


def iota(shape, dim):
    return lax.broadcasted_iota(I32, shape, dim)


def hot(cond):
    return jnp.where(cond, 1.0, 0.0).astype(BF16)


def dot(a, b):
    return jnp.dot(a, b, preferred_element_type=F32)


def pack_kernel(sdf, weight, color, voxel, valid, count, key, table, send, x, rows):
    key_row = key[...]
    high_hot = hot((key_row >> 7) == iota((64, LISTS), 0))
    low_hot = jnp.where((key_row & 127) == iota((128, LISTS), 0), 1.0, 0.0)
    slots = table[...]
    owner_of = (slots >> 6).astype(F32).T.astype(BF16)
    row_of = (slots & 63).astype(F32).T.astype(BF16)
    owner = jnp.sum(dot(owner_of, high_hot) * low_hot, axis=0, keepdims=True)
    row = jnp.sum(dot(row_of, high_hot) * low_hot, axis=0, keepdims=True)
    owner_hot = jnp.where(owner.astype(I32) == iota((DEVICES, LISTS), 0), 1.0, 0.0)
    before = hot(iota((LISTS, LISTS), 0) < iota((LISTS, LISTS), 1))
    order = jnp.sum(dot(owner_hot.astype(BF16), before) * owner_hot, axis=0, keepdims=True)

    diagonal = iota((LISTS, LISTS), 0) == iota((LISTS, LISTS), 1)
    spread = jnp.where(diagonal, count[...].astype(F32), 0.0).astype(BF16)
    used = dot(spread, jnp.ones((LISTS, PTS), BF16))
    live = (iota((LISTS, PTS), 1).astype(F32) < used) & (valid[...] == 1)
    mask = jnp.where(live, 1.0, 0.0)
    live_count = lax.dot_general(
        jnp.ones((8, PTS), BF16), mask.astype(BF16), NT, preferred_element_type=F32
    )[0:1]
    empty = jnp.zeros((1, META - LISTS), F32)
    lines = []
    for line in (
        jnp.concatenate([owner, empty - 1.0], axis=1),
        jnp.concatenate([row, empty], axis=1),
        jnp.concatenate([live_count, empty], axis=1),
    ):
        lines += [line[:, 0:128], line[:, 128:256]]
    head = jnp.concatenate(lines + [jnp.zeros((2, 128), F32)], axis=0)

    def spread_head(i, carry):
        rows[pl.ds(pl.multiple_of(i * ROWS + DATA, 8), 8), :] = head
        return carry

    lax.fori_loop(0, DEVICES, spread_head, 0, unroll=8)

    scaled = mask * weight[...]
    values = [
        (voxel[...] - 256).astype(F32),
        scaled,
        scaled * sdf[...],
        scaled * color[0],
        scaled * color[1],
        scaled * color[2],
    ]
    for v, value in enumerate(values):
        value = value.astype(BF16)
        for half in range(2):
            j = half * VALUES + v
            x[:, j * 128 : (j + 1) * 128] = value[:, half * 128 : (half + 1) * 128]

    for k in range(CAP):
        place = jnp.where(order == k, owner_hot, 0.0).astype(BF16)
        for j in range(0, 2 * VALUES, 2):
            moved = dot(place, x[:, j * 128 : (j + 2) * 128])
            for side in range(2):
                at = k * 2 * VALUES + j + side
                rows[pl.ds(at, DEVICES, stride=ROWS), :] = moved[
                    :, side * 128 : (side + 1) * 128
                ]

    def convert(i, carry):
        at = pl.multiple_of(i * ROWS, ROWS)
        send[pl.ds(at, ROWS), :] = rows[pl.ds(at, ROWS), :].astype(BF16)
        return carry

    lax.fori_loop(0, DEVICES, convert, 0, unroll=4)


def join_kernel(got, tsdf, color, counts, total, work, info, heads, heads_smem, sem):
    me = lax.axis_index("view") * 16 + lax.axis_index("tile")

    def unpack_head(i, carry):
        info[pl.ds(pl.multiple_of(i * 8, 8), 8), :] = got[i, DATA:ROWS, :].astype(F32)
        return carry

    lax.fori_loop(0, DEVICES, unpack_head, 0, unroll=8)

    def plane(p):
        return jnp.concatenate(
            [info[pl.ds(2 * p + half, DEVICES, stride=8), :] for half in range(2)], axis=1
        )

    mine = jnp.where(plane(0) == me.astype(F32), 1.0, 0.0)
    row = plane(1) + 1.0
    before = hot(iota((META, META), 0) < iota((META, META), 1))
    order = dot(mine.astype(BF16), before)
    found = jnp.zeros((8, DEVICES), F32)
    for k in range(CAP):
        picked = jnp.where((order == k) & (mine > 0.0), row, 0.0).astype(BF16)
        select = hot(iota((8, META), 0) == k)
        found += lax.dot_general(select, picked, NT, preferred_element_type=F32)
    found = found.astype(I32)
    heads[...] = jnp.where(found == 0, BLOCKS, found - 1) * STRIDE
    copy = pltpu.make_async_copy(heads, heads_smem, sem)
    copy.start()

    total[...] = jnp.zeros_like(total)
    work[...] = jnp.zeros_like(work)

    def tally(s, sums):
        line = info[pl.ds(pl.multiple_of(s * 8, 8), 8), :]

        def value(p):
            return jnp.concatenate([line[2 * p : 2 * p + 1], line[2 * p + 1 : 2 * p + 2]], axis=1)

        owner = value(0).astype(I32)
        low = (owner & 1) * BLOCKS + value(1).astype(I32)
        a = jnp.where((owner >> 1) == iota((64, META), 0), value(2), 0.0).astype(BF16)
        b = hot(low == iota((128, META), 0))
        return sums + lax.dot_general(a, b, NT, preferred_element_type=F32)

    sums = lax.fori_loop(0, DEVICES, tally, jnp.zeros((64, 128), F32), unroll=4)
    counts[...] = sums.astype(I32)
    copy.wait()

    low_id = iota((LOW, 128), 0).astype(F32)

    def body(i, carry):
        for src in range(SOURCES):
            base = src * WORK
            work[base : base + DATA, :] = got[i * SOURCES + src, 0:DATA, :].astype(F32)
        parts = []
        for src in range(SOURCES):
            for k in range(CAP):
                a_parts, b_parts = [], []
                for half in range(2):
                    at = src * WORK + (2 * k + half) * VALUES
                    index = jnp.broadcast_to(work[at : at + 1, :], (8, 128))
                    high = jnp.floor(index * (1.0 / LOW))
                    low = index - high * LOW
                    low_all = jnp.concatenate([low] * (LOW // 8), axis=0)
                    b_parts.append(jnp.where(low_all == low_id, 1.0, 0.0))
                    group = work[at : at + 8, :]
                    a_parts.append(
                        jnp.concatenate(
                            [jnp.where(high == float(h - 4), group, 0.0) for h in range(HIGH)],
                            axis=0,
                        )
                    )
                a = jnp.concatenate(a_parts, axis=1).astype(BF16)
                b = jnp.concatenate(b_parts, axis=1).astype(BF16)
                part = lax.dot_general(a, b, NT, preferred_element_type=F32)
                at = pl.multiple_of(heads_smem[k, i * SOURCES + src], 8)
                total[pl.ds(at, HIGH * 8), 0:LOW] += part
        return carry

    lax.fori_loop(0, DEVICES // SOURCES, body, 0)

    for h in range(HIGH):

        def channel(c):
            return total[pl.ds(h * 8 + c, BLOCKS, stride=STRIDE), :][:, 0:LOW]

        span = slice(h * LOW, (h + 1) * LOW)
        divisor = jnp.maximum(channel(1), 1.0)
        tsdf[:, span] = channel(2) / divisor
        for c in range(3):
            color[c, :, span] = channel(3 + c) / divisor


def on_device(sdf_value, weight, color, voxel_index, valid, list_count, list_key, owner_slot):
    send = pl.pallas_call(
        pack_kernel,
        out_shape=jax.ShapeDtypeStruct((DEVICES * ROWS, 128), BF16),
        in_specs=[VMEM] * 8,
        out_specs=VMEM,
        scratch_shapes=[
            pltpu.VMEM((LISTS, 2 * VALUES * 128), BF16),
            pltpu.VMEM((DEVICES * ROWS, 128), F32),
        ],
        compiler_params=pltpu.CompilerParams(vmem_limit_bytes=20 * 2**20),
        name="pack",
    )(
        *(
            pltpu.with_memory_space_constraint(given, pltpu.HBM)
            for given in (
                sdf_value,
                weight,
                color,
                voxel_index,
                valid,
                list_count.reshape(1, LISTS),
                list_key.reshape(1, LISTS),
                owner_slot.reshape(64, 128),
            )
        )
    )
    got = lax.all_to_all(
        send.reshape(DEVICES, ROWS, 128), AXES, split_axis=0, concat_axis=0, tiled=True
    )
    got = pltpu.with_memory_space_constraint(got, pltpu.VMEM)
    tsdf, colors, counts = pl.pallas_call(
        join_kernel,
        out_shape=(
            jax.ShapeDtypeStruct((BLOCKS, 512), F32),
            jax.ShapeDtypeStruct((3, BLOCKS, 512), F32),
            jax.ShapeDtypeStruct((64, 128), I32),
        ),
        in_specs=[VMEM],
        out_specs=(VMEM, VMEM, VMEM),
        scratch_shapes=[
            pltpu.VMEM(((BLOCKS + 1) * STRIDE, 128), F32),
            pltpu.VMEM((SOURCES * WORK, 128), F32),
            pltpu.VMEM((DEVICES * 8, 128), F32),
            pltpu.VMEM((8, DEVICES), I32),
            pltpu.SMEM((8, DEVICES), I32),
            pltpu.SemaphoreType.DMA,
        ],
        compiler_params=pltpu.CompilerParams(vmem_limit_bytes=20 * 2**20),
        name="join",
    )(got)
    return tsdf, jnp.transpose(colors, (1, 0, 2)), counts.reshape(DEVICES * BLOCKS)


def solution(mesh):
    return jax.shard_map(
        on_device,
        mesh=mesh,
        in_specs=(
            P(AXES, None),
            P(AXES, None),
            P(None, AXES, None),
            P(AXES, None),
            P(AXES, None),
            P(AXES),
            P(AXES),
            P(),
        ),
        out_specs=(P(AXES, None), P(AXES, None, None), P()),
        check_vma=False,
    )
```

time: 135 us -> 78 us (0.58)
  blocking collectives: 75.9 us -> 46.6 us
  Pallas kernels: 45 us -> 30.6 us
  starting transfers between devices: 11.5 us -> 0 us
  local copies, waits for them, and re-layouts: 2.08 us -> 0 us
    all_gather x1 -> x0, blocking collectives: 75.9 us -> none  [on_device(): gathered = lax.all_gather(meta, AXES, axis=0, tiled=True)]
    all_to_all x0 -> x1, blocking collectives: none -> 46.6 us  [on_device(): lax.all_to_all(send.reshape(DEVICES, ROWS, 128), AXES, split_axis=0, conc...]
    pallas_call x3 -> x2, Pallas kernels: 45 us -> 30.6 us  [the longest x1 26.6 us: on_device(): pl.pallas_call(join_kernel, out_shape=(jax.ShapeDtypeStruct((BLOCKS, 512)...]
    all_to_all x1 -> x0, starting transfers between devices: 11.5 us -> none  [on_device(): lax.all_to_all(send.reshape(DEVICES, ROWS, 128), AXES, split_axis=0, conc...]
    unnamed x5 -> x0, local copies, waits for them, and re-layouts: 2.08 us -> none
  transfers between devices with their start and end apart: 1 -> 0, of which waited for: 0 -> 0; matrix products, arithmetic and copies ran while one was open for 0% -> 0% of each run, Pallas kernels for 7% -> 0%
where the time goes in v2:
time: 78 us; the launch traced here: 77.9 us
  blocking collectives  46.6 us (60%)
  Pallas kernels  30.6 us (39%)
    all_to_all x1, blocking collectives, on_device(): lax.all_to_all(send.reshape(DEVICES, ROWS, 128), AXES, split_axis=0, conc...  46.6 us
    pallas_call x1, Pallas kernels, on_device(): pl.pallas_call(join_kernel, out_shape=(jax.ShapeDtypeStruct((BLOCKS, 512)...  26.6 us
    pallas_call x1, Pallas kernels, on_device(): pl.pallas_call(pack_kernel, out_shape=jax.ShapeDtypeStruct((DEVICES * ROW...  3.97 us

profile of v2, /device:TPU:1, one launch (start us, length us, event | category | flops | bytes accessed | tf_op | source)
XLA Modules:
  0.0 77.9 jit_solution(13481449664980636299)
XLA Ops:
  0.6 4.0 %pack.1 = bf16[10240,128]{1,0:T(8,128)(2,1)S(1)} custom-call(f32[192,256]{1,0:T(8,128)} %sdf.1, f32[192,256]{1,0:T(8,128)} %weight.1, f32[3,192,256]{2,1,0:T(8,128)} %color.1, s32[192,256]{1,0:T(8,128)} %voxel.1, s32[192,256]{1,0:T(8,128)} %valid.1, s32[1,192]{1,0:T(1,128)} %bitcast.8, s32[1,192]{1,0:T(1,128)} %bitcast.9, s32[64,128]{1,0:T(8,128)} %bitcast.7), custom_call_target="tpu_custom_call" | custom-call | tf_op jit(solution)/shard_map/pack/pallas_call | solution.py:205
  4.6 46.6 %all_to_all.5.got = bf16[128,80,128]{2,1,0:T(8,128)(2,1)S(1)} all-to-all(bf16[128,80,128]{2,1,0:T(8,128)(2,1)S(1)} %bitcast.6), channel_id=1, replica_groups=mesh['view'=8,'tile'=16] {'view','tile'}, dimensions={0} | all-to-all | bytes 5242880 | tf_op jit(solution)/shard_map/all_to_all | solution.py:231
  51.3 26.6 %join.1 = (f32[64,512]{1,0:T(8,128)}, f32[3,64,512]{2,1,0:T(8,128)}, s32[64,128]{1,0:T(8,128)}) custom-call(bf16[128,80,128]{2,1,0:T(8,128)(2,1)S(1)} %all_to_all.5.got), custom_call_target="tpu_custom_call" | custom-call | tf_op jit(solution)/shard_map/join/pallas_call | solution.py:235

commit v3 on v2

--- a/solution.py
+++ b/solution.py
@@ -18,7 +18,9 @@
 LOW = 64
 STRIDE = 72
 META = 256
-SOURCES = 2
+SOURCES = 16
+TALLY = DEVICES * LISTS // 128
+GROUP = 32
 WORK = 80
 F32 = jnp.float32
 BF16 = jnp.bfloat16
@@ -60,14 +62,21 @@
     live_count = lax.dot_general(
         jnp.ones((8, PTS), BF16), mask.astype(BF16), NT, preferred_element_type=F32
     )[0:1]
-    empty = jnp.zeros((1, META - LISTS), F32)
+    storage = owner * BLOCKS + row
+    high = jnp.floor(storage * (1.0 / 128))
+    odd = (lax.axis_index("tile") & 1) == 1
     lines = []
-    for line in (
-        jnp.concatenate([owner, empty - 1.0], axis=1),
-        jnp.concatenate([row, empty], axis=1),
-        jnp.concatenate([live_count, empty], axis=1),
-    ):
-        lines += [line[:, 0:128], line[:, 128:256]]
+    for line, fill in ((high, -1.0), (storage - high * 128, 0.0), (live_count, 0.0)):
+        blank = jnp.full((1, 64), fill, F32)
+        rest = line[:, 128:LISTS]
+        lines += [
+            line[:, 0:128],
+            jnp.where(
+                odd,
+                jnp.concatenate([blank, rest], axis=1),
+                jnp.concatenate([rest, blank], axis=1),
+            ),
+        ]
     head = jnp.concatenate(lines + [jnp.zeros((2, 128), F32)], axis=0)
 
     def spread_head(i, carry):
@@ -109,27 +118,36 @@
     lax.fori_loop(0, DEVICES, convert, 0, unroll=4)
 
 
-def join_kernel(got, tsdf, color, counts, total, work, info, heads, heads_smem, sem):
+def twice(rows8):
+    return jnp.concatenate([rows8, rows8], axis=0).astype(BF16)
+
+
+def ids(count):
+    return [(iota((16, 128), 0) + 16 * j).astype(F32).astype(BF16) for j in range(count)]
+
+
+def join_kernel(got, tsdf, color, counts, total, work, info, lines, heads, heads_smem, sem):
     me = lax.axis_index("view") * 16 + lax.axis_index("tile")
+    one, zero = jnp.ones((), BF16), jnp.zeros((), BF16)
 
     def unpack_head(i, carry):
         info[pl.ds(pl.multiple_of(i * 8, 8), 8), :] = got[i, DATA:ROWS, :].astype(F32)
         return carry
 
-    lax.fori_loop(0, DEVICES, unpack_head, 0, unroll=8)
+    lax.fori_loop(0, DEVICES, unpack_head, 0, unroll=16)
 
     def plane(p):
         return jnp.concatenate(
             [info[pl.ds(2 * p + half, DEVICES, stride=8), :] for half in range(2)], axis=1
         )
 
-    mine = jnp.where(plane(0) == me.astype(F32), 1.0, 0.0)
-    row = plane(1) + 1.0
+    row = plane(0) * 128.0 + plane(1) - (me * BLOCKS).astype(F32)
+    mine = (row >= 0.0) & (row < float(BLOCKS))
     before = hot(iota((META, META), 0) < iota((META, META), 1))
-    order = dot(mine.astype(BF16), before)
+    order = dot(hot(mine), before)
     found = jnp.zeros((8, DEVICES), F32)
     for k in range(CAP):
-        picked = jnp.where((order == k) & (mine > 0.0), row, 0.0).astype(BF16)
+        picked = jnp.where((order == k) & mine, row + 1.0, 0.0).astype(BF16)
         select = hot(iota((8, META), 0) == k)
         found += lax.dot_general(select, picked, NT, preferred_element_type=F32)
     found = found.astype(I32)
@@ -140,29 +158,46 @@
     total[...] = jnp.zeros_like(total)
     work[...] = jnp.zeros_like(work)
 
-    def tally(s, sums):
-        line = info[pl.ds(pl.multiple_of(s * 8, 8), 8), :]
-
-        def value(p):
-            return jnp.concatenate([line[2 * p : 2 * p + 1], line[2 * p + 1 : 2 * p + 2]], axis=1)
-
-        owner = value(0).astype(I32)
-        low = (owner & 1) * BLOCKS + value(1).astype(I32)
-        a = jnp.where((owner >> 1) == iota((64, META), 0), value(2), 0.0).astype(BF16)
-        b = hot(low == iota((128, META), 0))
+    left = iota((DEVICES // 2, 128), 1) < 64
+    for p in range(3):
+        lines[p, 0:DEVICES, :] = info[pl.ds(2 * p, DEVICES, stride=8), :]
+        lines[p, DEVICES:TALLY, :] = jnp.where(
+            left,
+            info[pl.ds(2 * p + 1, DEVICES // 2, stride=16), :],
+            info[pl.ds(2 * p + 9, DEVICES // 2, stride=16), :],
+        )
+    tally_ids = ids(8)
+
+    def tally(g, sums):
+        a_parts, b_parts = [], []
+        for t in range(GROUP):
+            high, low, number = [
+                twice(jnp.broadcast_to(lines[p, pl.ds(g * GROUP + t, 1), :], (8, 128)))
+                for p in range(3)
+            ]
+            a_parts.append(
+                jnp.concatenate([jnp.where(high == tally_ids[j], number, zero) for j in range(4)], 0)
+            )
+            b_parts.append(
+                jnp.concatenate([jnp.where(low == tally_ids[j], one, zero) for j in range(8)], 0)
+            )
+        a = jnp.concatenate(a_parts, axis=1)
+        b = jnp.concatenate(b_parts, axis=1)
         return sums + lax.dot_general(a, b, NT, preferred_element_type=F32)
 
-    sums = lax.fori_loop(0, DEVICES, tally, jnp.zeros((64, 128), F32), unroll=4)
+    sums = lax.fori_loop(0, TALLY // GROUP, tally, jnp.zeros((64, 128), F32))
     counts[...] = sums.astype(I32)
     copy.wait()
 
-    low_id = iota((LOW, 128), 0).astype(F32)
+    low_id = iota((LOW, 128), 0).astype(F32).astype(BF16)
+    high_id = [
+        ((iota((16, 128), 0) >> 3) + (2 * j - 4)).astype(F32).astype(BF16) for j in range(HIGH // 2)
+    ]
 
     def body(i, carry):
         for src in range(SOURCES):
             base = src * WORK
             work[base : base + DATA, :] = got[i * SOURCES + src, 0:DATA, :].astype(F32)
-        parts = []
         for src in range(SOURCES):
             for k in range(CAP):
                 a_parts, b_parts = [], []
@@ -170,18 +205,19 @@
                     at = src * WORK + (2 * k + half) * VALUES
                     index = jnp.broadcast_to(work[at : at + 1, :], (8, 128))
                     high = jnp.floor(index * (1.0 / LOW))
-                    low = index - high * LOW
-                    low_all = jnp.concatenate([low] * (LOW // 8), axis=0)
-                    b_parts.append(jnp.where(low_all == low_id, 1.0, 0.0))
-                    group = work[at : at + 8, :]
+                    low = twice(index - high * LOW)
+                    high = twice(high)
+                    low_all = jnp.concatenate([low] * (LOW // 16), axis=0)
+                    b_parts.append(jnp.where(low_all == low_id, one, zero))
+                    group = twice(work[at : at + 8, :])
                     a_parts.append(
                         jnp.concatenate(
-                            [jnp.where(high == float(h - 4), group, 0.0) for h in range(HIGH)],
+                            [jnp.where(high == high_id[j], group, zero) for j in range(HIGH // 2)],
                             axis=0,
                         )
                     )
-                a = jnp.concatenate(a_parts, axis=1).astype(BF16)
-                b = jnp.concatenate(b_parts, axis=1).astype(BF16)
+                a = jnp.concatenate(a_parts, axis=1)
+                b = jnp.concatenate(b_parts, axis=1)
                 part = lax.dot_general(a, b, NT, preferred_element_type=F32)
                 at = pl.multiple_of(heads_smem[k, i * SOURCES + src], 8)
                 total[pl.ds(at, HIGH * 8), 0:LOW] += part
@@ -201,8 +237,8 @@
             color[c, :, span] = channel(3 + c) / divisor
 
 
-def on_device(sdf_value, weight, color, voxel_index, valid, list_count, list_key, owner_slot):
-    send = pl.pallas_call(
+def pack(sdf_value, weight, color, voxel_index, valid, list_count, list_key, owner_slot):
+    return pl.pallas_call(
         pack_kernel,
         out_shape=jax.ShapeDtypeStruct((DEVICES * ROWS, 128), BF16),
         in_specs=[VMEM] * 8,
@@ -228,11 +264,10 @@
             )
         )
     )
-    got = lax.all_to_all(
-        send.reshape(DEVICES, ROWS, 128), AXES, split_axis=0, concat_axis=0, tiled=True
-    )
-    got = pltpu.with_memory_space_constraint(got, pltpu.VMEM)
-    tsdf, colors, counts = pl.pallas_call(
+
+
+def join(got):
+    return pl.pallas_call(
         join_kernel,
         out_shape=(
             jax.ShapeDtypeStruct((BLOCKS, 512), F32),
@@ -245,13 +280,21 @@
             pltpu.VMEM(((BLOCKS + 1) * STRIDE, 128), F32),
             pltpu.VMEM((SOURCES * WORK, 128), F32),
             pltpu.VMEM((DEVICES * 8, 128), F32),
+            pltpu.VMEM((3, TALLY, 128), F32),
             pltpu.VMEM((8, DEVICES), I32),
             pltpu.SMEM((8, DEVICES), I32),
             pltpu.SemaphoreType.DMA,
         ],
         compiler_params=pltpu.CompilerParams(vmem_limit_bytes=20 * 2**20),
         name="join",
-    )(got)
+    )(pltpu.with_memory_space_constraint(got, pltpu.VMEM))
+
+
+def on_device(*given):
+    got = lax.all_to_all(
+        pack(*given).reshape(DEVICES, ROWS, 128), AXES, split_axis=0, concat_axis=0, tiled=True
+    )
+    tsdf, colors, counts = join(got)
     return tsdf, jnp.transpose(colors, (1, 0, 2)), counts.reshape(DEVICES * BLOCKS)
 
 

time: 78 us -> 64.2 us (0.82)
  Pallas kernels: 30.6 us -> 16.8 us
    pallas_call x2, Pallas kernels: 30.6 us -> 16.8 us  [the longest x1 12.7 us: join(): pl.pallas_call(join_kernel, out_shape=(jax.ShapeDtypeStruct((BLOCKS, 512)...]
where the time goes in v3:
time: 64.2 us; the launch traced here: 64.1 us
  blocking collectives  46.6 us (73%)
  Pallas kernels  16.8 us (26%)
    all_to_all x1, blocking collectives, on_device(): lax.all_to_all(pack(*given).reshape(DEVICES, ROWS, 128), AXES, split_axis...  46.6 us
    pallas_call x1, Pallas kernels, join(): pl.pallas_call(join_kernel, out_shape=(jax.ShapeDtypeStruct((BLOCKS, 512)...  12.7 us
    pallas_call x1, Pallas kernels, pack(): pl.pallas_call(pack_kernel, out_shape=jax.ShapeDtypeStruct((DEVICES * ROW...  4.04 us

profile of v3, /device:TPU:1, one launch (start us, length us, event | category | flops | bytes accessed | tf_op | source)
XLA Modules:
  0.0 64.1 jit_solution(14434124907802385815)
XLA Ops:
  0.6 4.0 %pack.1 = bf16[10240,128]{1,0:T(8,128)(2,1)S(1)} custom-call(f32[192,256]{1,0:T(8,128)} %sdf.1, f32[192,256]{1,0:T(8,128)} %weight.1, f32[3,192,256]{2,1,0:T(8,128)} %color.1, s32[192,256]{1,0:T(8,128)} %voxel.1, s32[192,256]{1,0:T(8,128)} %valid.1, s32[1,192]{1,0:T(1,128)} %bitcast.8, s32[1,192]{1,0:T(1,128)} %bitcast.9, s32[64,128]{1,0:T(8,128)} %bitcast.7), custom_call_target="tpu_custom_call" | custom-call | tf_op jit(solution)/shard_map/pack/pallas_call | solution.py:241
  4.7 46.6 %all_to_all.5.got = bf16[128,80,128]{2,1,0:T(8,128)(2,1)S(1)} all-to-all(bf16[128,80,128]{2,1,0:T(8,128)(2,1)S(1)} %bitcast.6), channel_id=1, replica_groups=mesh['view'=8,'tile'=16] {'view','tile'}, dimensions={0} | all-to-all | bytes 5242880 | tf_op jit(solution)/shard_map/all_to_all | solution.py:294
  51.3 12.7 %join.1 = (f32[64,512]{1,0:T(8,128)}, f32[3,64,512]{2,1,0:T(8,128)}, s32[64,128]{1,0:T(8,128)}) custom-call(bf16[128,80,128]{2,1,0:T(8,128)(2,1)S(1)} %all_to_all.5.got), custom_call_target="tpu_custom_call" | custom-call | tf_op jit(solution)/shard_map/join/pallas_call | solution.py:270

commit v4 on v3

--- a/solution.py
+++ b/solution.py
@@ -17,8 +17,9 @@
 HIGH = 8
 LOW = 64
 STRIDE = 72
+SPREAD = 84
 META = 256
-SOURCES = 16
+SOURCES = 32
 TALLY = DEVICES * LISTS // 128
 GROUP = 32
 WORK = 80
@@ -41,7 +42,18 @@
     return jnp.dot(a, b, preferred_element_type=F32)
 
 
-def pack_kernel(sdf, weight, color, voxel, valid, count, key, table, send, x, rows):
+def pack_kernel(*refs):
+    given, send, x, rows, place = refs[:8], refs[8], refs[9], refs[10], refs[11]
+    held, sems = refs[12:20], refs[20]
+    copies = [
+        pltpu.make_async_copy(src, dst, sems.at[i]) for i, (src, dst) in enumerate(zip(given, held))
+    ]
+    for copy in copies:
+        copy.start()
+    key, table, count, valid, voxel, weight, sdf, color = held
+
+    copies[0].wait()
+    copies[1].wait()
     key_row = key[...]
     high_hot = hot((key_row >> 7) == iota((64, LISTS), 0))
     low_hot = jnp.where((key_row & 127) == iota((128, LISTS), 0), 1.0, 0.0)
@@ -53,7 +65,13 @@
     owner_hot = jnp.where(owner.astype(I32) == iota((DEVICES, LISTS), 0), 1.0, 0.0)
     before = hot(iota((LISTS, LISTS), 0) < iota((LISTS, LISTS), 1))
     order = jnp.sum(dot(owner_hot.astype(BF16), before) * owner_hot, axis=0, keepdims=True)
-
+    for k in range(CAP):
+        place[k * DEVICES : (k + 1) * DEVICES, :] = jnp.where(order == k, owner_hot, 0.0).astype(
+            BF16
+        )
+
+    copies[2].wait()
+    copies[3].wait()
     diagonal = iota((LISTS, LISTS), 0) == iota((LISTS, LISTS), 1)
     spread = jnp.where(diagonal, count[...].astype(F32), 0.0).astype(BF16)
     used = dot(spread, jnp.ones((LISTS, PTS), BF16))
@@ -80,11 +98,13 @@
     head = jnp.concatenate(lines + [jnp.zeros((2, 128), F32)], axis=0)
 
     def spread_head(i, carry):
-        rows[pl.ds(pl.multiple_of(i * ROWS + DATA, 8), 8), :] = head
+        rows[pl.ds(i * SPREAD + DATA, 8), :] = head
         return carry
 
     lax.fori_loop(0, DEVICES, spread_head, 0, unroll=8)
 
+    for copy in copies[4:]:
+        copy.wait()
     scaled = mask * weight[...]
     values = [
         (voxel[...] - 256).astype(F32),
@@ -100,22 +120,19 @@
             j = half * VALUES + v
             x[:, j * 128 : (j + 1) * 128] = value[:, half * 128 : (half + 1) * 128]
 
-    for k in range(CAP):
-        place = jnp.where(order == k, owner_hot, 0.0).astype(BF16)
-        for j in range(0, 2 * VALUES, 2):
-            moved = dot(place, x[:, j * 128 : (j + 2) * 128])
+    for j in range(0, 2 * VALUES, 2):
+        for k in range(CAP):
+            moved = dot(place[k * DEVICES : (k + 1) * DEVICES, :], x[:, j * 128 : (j + 2) * 128])
             for side in range(2):
                 at = k * 2 * VALUES + j + side
-                rows[pl.ds(at, DEVICES, stride=ROWS), :] = moved[
-                    :, side * 128 : (side + 1) * 128
-                ]
+                rows[pl.ds(at, DEVICES, stride=SPREAD), :] = moved[:, side * 128 : (side + 1) * 128]
 
     def convert(i, carry):
         at = pl.multiple_of(i * ROWS, ROWS)
-        send[pl.ds(at, ROWS), :] = rows[pl.ds(at, ROWS), :].astype(BF16)
+        send[pl.ds(at, ROWS), :] = rows[pl.ds(i * SPREAD, ROWS), :].astype(BF16)
         return carry
 
-    lax.fori_loop(0, DEVICES, convert, 0, unroll=4)
+    lax.fori_loop(0, DEVICES, convert, 0, unroll=8)
 
 
 def twice(rows8):
@@ -238,32 +255,31 @@
 
 
 def pack(sdf_value, weight, color, voxel_index, valid, list_count, list_key, owner_slot):
+    given = (
+        list_key.reshape(1, LISTS),
+        owner_slot.reshape(64, 128),
+        list_count.reshape(1, LISTS),
+        valid,
+        voxel_index,
+        weight,
+        sdf_value,
+        color,
+    )
     return pl.pallas_call(
         pack_kernel,
         out_shape=jax.ShapeDtypeStruct((DEVICES * ROWS, 128), BF16),
-        in_specs=[VMEM] * 8,
+        in_specs=[pl.BlockSpec(memory_space=pl.ANY)] * 8,
         out_specs=VMEM,
         scratch_shapes=[
             pltpu.VMEM((LISTS, 2 * VALUES * 128), BF16),
-            pltpu.VMEM((DEVICES * ROWS, 128), F32),
+            pltpu.VMEM((DEVICES * SPREAD, 128), F32),
+            pltpu.VMEM((CAP * DEVICES, LISTS), BF16),
+            *(pltpu.VMEM(array.shape, array.dtype) for array in given),
+            pltpu.SemaphoreType.DMA((8,)),
         ],
         compiler_params=pltpu.CompilerParams(vmem_limit_bytes=20 * 2**20),
         name="pack",
-    )(
-        *(
-            pltpu.with_memory_space_constraint(given, pltpu.HBM)
-            for given in (
-                sdf_value,
-                weight,
-                color,
-                voxel_index,
-                valid,
-                list_count.reshape(1, LISTS),
-                list_key.reshape(1, LISTS),
-                owner_slot.reshape(64, 128),
-            )
-        )
-    )
+    )(*(pltpu.with_memory_space_constraint(array, pltpu.HBM) for array in given))
 
 
 def join(got):

time: 64.2 us -> 62.6 us (0.975)
  Pallas kernels: 16.8 us -> 15.2 us
    pallas_call x1, Pallas kernels: 4.04 us -> 2.88 us  [pack(): pl.pallas_call(pack_kernel, out_shape=jax.ShapeDtypeStruct((DEVICES * ROW...]
where the time goes in v4:
time: 62.6 us; the launch traced here: 62.5 us
  blocking collectives  46.6 us (74%)
  Pallas kernels  15.2 us (24%)
  between operations  0.64 us (1%)
    all_to_all x1, blocking collectives, on_device(): lax.all_to_all(pack(*given).reshape(DEVICES, ROWS, 128), AXES, split_axis...  46.6 us
    pallas_call x1, Pallas kernels, join(): pl.pallas_call(join_kernel, out_shape=(jax.ShapeDtypeStruct((BLOCKS, 512)...  12.3 us
    pallas_call x1, Pallas kernels, pack(): pl.pallas_call(pack_kernel, out_shape=jax.ShapeDtypeStruct((DEVICES * ROW...  2.88 us

profile of v4, /device:TPU:1, one launch (start us, length us, event | category | flops | bytes accessed | tf_op | source)
XLA Modules:
  0.0 62.5 jit_solution(1835241593333697092)
XLA Ops:
  0.6 2.9 %pack.1 = bf16[10240,128]{1,0:T(8,128)(2,1)S(1)} custom-call(s32[1,192]{1,0:T(1,128)} %bitcast.8, s32[64,128]{1,0:T(8,128)} %bitcast.7, s32[1,192]{1,0:T(1,128)} %bitcast.9, s32[192,256]{1,0:T(8,128)} %refs_3_.1, s32[192,256]{1,0:T(8,128)} %refs_4_.1, f32[192,256]{1,0:T(8,128)} %refs_5_.1, f32[192,256]{1,0:T(8,128)} %refs_6_.1, f32[3,192,256]{2,1,0:T(8,128)} %refs_7_.1), custom_call_target="tpu_custom_call" | custom-call | tf_op jit(solution)/shard_map/pack/pallas_call | solution.py:268
  3.5 46.6 %all_to_all.5.got = bf16[128,80,128]{2,1,0:T(8,128)(2,1)S(1)} all-to-all(bf16[128,80,128]{2,1,0:T(8,128)(2,1)S(1)} %bitcast.6), channel_id=1, replica_groups=mesh['view'=8,'tile'=16] {'view','tile'}, dimensions={0} | all-to-all | bytes 5242880 | tf_op jit(solution)/shard_map/all_to_all | solution.py:310
  50.2 12.3 %join.1 = (f32[64,512]{1,0:T(8,128)}, f32[3,64,512]{2,1,0:T(8,128)}, s32[64,128]{1,0:T(8,128)}) custom-call(bf16[128,80,128]{2,1,0:T(8,128)(2,1)S(1)} %all_to_all.5.got), custom_call_target="tpu_custom_call" | custom-call | tf_op jit(solution)/shard_map/join/pallas_call | solution.py:286

commit v5 on v4

--- a/solution.py
+++ b/solution.py
@@ -13,16 +13,16 @@
 CAP = 6
 VALUES = 6
 DATA = CAP * VALUES * 2
-ROWS = DATA + 8
+ROWS = DATA + 4
+PAIR = 2 * ROWS
+GAP = 20
 HIGH = 8
 LOW = 64
 STRIDE = 72
-SPREAD = 84
 META = 256
 SOURCES = 32
 TALLY = DEVICES * LISTS // 128
 GROUP = 32
-WORK = 80
 F32 = jnp.float32
 BF16 = jnp.bfloat16
 I32 = jnp.int32
@@ -82,10 +82,14 @@
     )[0:1]
     storage = owner * BLOCKS + row
     high = jnp.floor(storage * (1.0 / 128))
+    code = storage - high * 128.0 + 128.0
+    high_bits = high.astype(I32)
+    for bit in range(6):
+        code = jnp.where((high_bits >> bit) & 1 == 1, code * 2.0 ** (1 << bit), code)
     odd = (lax.axis_index("tile") & 1) == 1
+    blank = jnp.zeros((1, 64), F32)
     lines = []
-    for line, fill in ((high, -1.0), (storage - high * 128, 0.0), (live_count, 0.0)):
-        blank = jnp.full((1, 64), fill, F32)
+    for line in (code, live_count):
         rest = line[:, 128:LISTS]
         lines += [
             line[:, 0:128],
@@ -95,10 +99,10 @@
                 jnp.concatenate([rest, blank], axis=1),
             ),
         ]
-    head = jnp.concatenate(lines + [jnp.zeros((2, 128), F32)], axis=0)
+    head = jnp.concatenate(lines, axis=0)
 
     def spread_head(i, carry):
-        rows[pl.ds(i * SPREAD + DATA, 8), :] = head
+        rows[pl.ds(i * ROWS + DATA, 4), :] = head
         return carry
 
     lax.fori_loop(0, DEVICES, spread_head, 0, unroll=8)
@@ -125,14 +129,14 @@
             moved = dot(place[k * DEVICES : (k + 1) * DEVICES, :], x[:, j * 128 : (j + 2) * 128])
             for side in range(2):
                 at = k * 2 * VALUES + j + side
-                rows[pl.ds(at, DEVICES, stride=SPREAD), :] = moved[:, side * 128 : (side + 1) * 128]
+                rows[pl.ds(at, DEVICES, stride=ROWS), :] = moved[:, side * 128 : (side + 1) * 128]
 
     def convert(i, carry):
-        at = pl.multiple_of(i * ROWS, ROWS)
-        send[pl.ds(at, ROWS), :] = rows[pl.ds(i * SPREAD, ROWS), :].astype(BF16)
+        at = pl.multiple_of(i * PAIR, PAIR)
+        send[pl.ds(at, PAIR), :] = rows[pl.ds(at, PAIR), :].astype(BF16)
         return carry
 
-    lax.fori_loop(0, DEVICES, convert, 0, unroll=8)
+    lax.fori_loop(0, DEVICES // 2, convert, 0, unroll=4)
 
 
 def twice(rows8):
@@ -148,17 +152,31 @@
     one, zero = jnp.ones((), BF16), jnp.zeros((), BF16)
 
     def unpack_head(i, carry):
-        info[pl.ds(pl.multiple_of(i * 8, 8), 8), :] = got[i, DATA:ROWS, :].astype(F32)
+        for side in range(2):
+            at = pl.multiple_of(i * PAIR + DATA * (side + 1), 8)
+            info[pl.ds(i * GAP + 8 * side, 8), :] = got[pl.ds(at, 8), :].astype(F32)
         return carry
 
-    lax.fori_loop(0, DEVICES, unpack_head, 0, unroll=16)
-
-    def plane(p):
+    lax.fori_loop(0, DEVICES // 2, unpack_head, 0, unroll=16)
+
+    def line(p):
         return jnp.concatenate(
-            [info[pl.ds(2 * p + half, DEVICES, stride=8), :] for half in range(2)], axis=1
+            [info[pl.ds(p + 12 * side, DEVICES // 2, stride=GAP), :] for side in range(2)], axis=0
         )
 
-    row = plane(0) * 128.0 + plane(1) - (me * BLOCKS).astype(F32)
+    def decoded(code):
+        high = jnp.zeros_like(code)
+        for bit in range(5, -1, -1):
+            step = float(1 << bit)
+            over = code >= 128.0 * 2.0**step
+            code = jnp.where(over, code * 2.0**-step, code)
+            high = jnp.where(over, high + step, high)
+        return high, code - 128.0
+
+    full = (*decoded(line(0)), line(2))
+    rest = (*decoded(line(1)), line(3))
+    row = jnp.concatenate([full[0] * 128.0 + full[1], rest[0] * 128.0 + rest[1]], axis=1)
+    row = row - (me * BLOCKS).astype(F32)
     mine = (row >= 0.0) & (row < float(BLOCKS))
     before = hot(iota((META, META), 0) < iota((META, META), 1))
     order = dot(hot(mine), before)
@@ -173,15 +191,12 @@
     copy.start()
 
     total[...] = jnp.zeros_like(total)
-    work[...] = jnp.zeros_like(work)
 
     left = iota((DEVICES // 2, 128), 1) < 64
     for p in range(3):
-        lines[p, 0:DEVICES, :] = info[pl.ds(2 * p, DEVICES, stride=8), :]
+        lines[p, 0:DEVICES, :] = full[p]
         lines[p, DEVICES:TALLY, :] = jnp.where(
-            left,
-            info[pl.ds(2 * p + 1, DEVICES // 2, stride=16), :],
-            info[pl.ds(2 * p + 9, DEVICES // 2, stride=16), :],
+            left, rest[p][0 : DEVICES // 2], rest[p][DEVICES // 2 : DEVICES]
         )
     tally_ids = ids(8)
 
@@ -212,14 +227,14 @@
     ]
 
     def body(i, carry):
-        for src in range(SOURCES):
-            base = src * WORK
-            work[base : base + DATA, :] = got[i * SOURCES + src, 0:DATA, :].astype(F32)
+        for pair in range(SOURCES // 2):
+            at = pl.multiple_of((i * (SOURCES // 2) + pair) * PAIR, 8)
+            work[pair * PAIR : (pair + 1) * PAIR, :] = got[pl.ds(at, PAIR), :].astype(F32)
         for src in range(SOURCES):
             for k in range(CAP):
                 a_parts, b_parts = [], []
                 for half in range(2):
-                    at = src * WORK + (2 * k + half) * VALUES
+                    at = src * ROWS + (2 * k + half) * VALUES
                     index = jnp.broadcast_to(work[at : at + 1, :], (8, 128))
                     high = jnp.floor(index * (1.0 / LOW))
                     low = twice(index - high * LOW)
@@ -236,7 +251,7 @@
                 a = jnp.concatenate(a_parts, axis=1)
                 b = jnp.concatenate(b_parts, axis=1)
                 part = lax.dot_general(a, b, NT, preferred_element_type=F32)
-                at = pl.multiple_of(heads_smem[k, i * SOURCES + src], 8)
+                at = pl.multiple_of(heads_smem[k, i * (SOURCES // 2) + src // 2 + src % 2 * (DEVICES // 2)], 8)
                 total[pl.ds(at, HIGH * 8), 0:LOW] += part
         return carry
 
@@ -272,7 +287,7 @@
         out_specs=VMEM,
         scratch_shapes=[
             pltpu.VMEM((LISTS, 2 * VALUES * 128), BF16),
-            pltpu.VMEM((DEVICES * SPREAD, 128), F32),
+            pltpu.VMEM((DEVICES * ROWS, 128), F32),
             pltpu.VMEM((CAP * DEVICES, LISTS), BF16),
             *(pltpu.VMEM(array.shape, array.dtype) for array in given),
             pltpu.SemaphoreType.DMA((8,)),
@@ -294,8 +309,8 @@
         out_specs=(VMEM, VMEM, VMEM),
         scratch_shapes=[
             pltpu.VMEM(((BLOCKS + 1) * STRIDE, 128), F32),
-            pltpu.VMEM((SOURCES * WORK, 128), F32),
-            pltpu.VMEM((DEVICES * 8, 128), F32),
+            pltpu.VMEM((SOURCES * ROWS, 128), F32),
+            pltpu.VMEM((DEVICES // 2 * GAP, 128), F32),
             pltpu.VMEM((3, TALLY, 128), F32),
             pltpu.VMEM((8, DEVICES), I32),
             pltpu.SMEM((8, DEVICES), I32),
@@ -307,10 +322,9 @@
 
 
 def on_device(*given):
-    got = lax.all_to_all(
-        pack(*given).reshape(DEVICES, ROWS, 128), AXES, split_axis=0, concat_axis=0, tiled=True
-    )
-    tsdf, colors, counts = join(got)
+    send = pack(*given).reshape(DEVICES, ROWS // 2, 2, 128)
+    got = lax.all_to_all(send, AXES, split_axis=0, concat_axis=0, tiled=True)
+    tsdf, colors, counts = join(got.reshape(DEVICES * ROWS, 128))
     return tsdf, jnp.transpose(colors, (1, 0, 2)), counts.reshape(DEVICES * BLOCKS)
 
 

time: 62.6 us -> 61.2 us (0.978)
  blocking collectives: 46.6 us -> 45.2 us
    all_to_all x1, blocking collectives: 46.6 us -> 45.2 us  [on_device(): got = lax.all_to_all(send, AXES, split_axis=0, concat_axis=0, tiled=True)]
where the time goes in v5:
time: 61.2 us; the launch traced here: 61 us
  blocking collectives  45.2 us (74%)
  Pallas kernels  15.2 us (25%)
  between operations  0.64 us (1%)
    all_to_all x1, blocking collectives, on_device(): got = lax.all_to_all(send, AXES, split_axis=0, concat_axis=0, tiled=True)  45.2 us
    pallas_call x1, Pallas kernels, join(): pl.pallas_call(join_kernel, out_shape=(jax.ShapeDtypeStruct((BLOCKS, 512)...  12.3 us
    pallas_call x1, Pallas kernels, pack(): pl.pallas_call(pack_kernel, out_shape=jax.ShapeDtypeStruct((DEVICES * ROW...  2.87 us

profile of v5, /device:TPU:1, one launch (start us, length us, event | category | flops | bytes accessed | tf_op | source)
XLA Modules:
  0.0 61.0 jit_solution(17526174661752072685)
XLA Ops:
  0.6 2.9 %pack.1 = bf16[9728,128]{1,0:T(8,128)(2,1)S(1)} custom-call(s32[1,192]{1,0:T(1,128)} %bitcast.10, s32[64,128]{1,0:T(8,128)} %bitcast.9, s32[1,192]{1,0:T(1,128)} %bitcast.11, s32[192,256]{1,0:T(8,128)} %refs_3_.1, s32[192,256]{1,0:T(8,128)} %refs_4_.1, f32[192,256]{1,0:T(8,128)} %refs_5_.1, f32[192,256]{1,0:T(8,128)} %refs_6_.1, f32[3,192,256]{2,1,0:T(8,128)} %refs_7_.1), custom_call_target="tpu_custom_call" | custom-call | tf_op jit(solution)/shard_map/pack/pallas_call | solution.py:283
  3.5 45.2 %all_to_all.5 = bf16[128,38,2,128]{3,2,1,0:T(2,128)(2,1)S(1)} all-to-all(bf16[128,38,2,128]{3,2,1,0:T(2,128)(2,1)S(1)} %bitcast.8), channel_id=1, replica_groups=mesh['view'=8,'tile'=16] {'view','tile'}, dimensions={0} | all-to-all | bytes 4980736 | tf_op jit(solution)/shard_map/all_to_all | solution.py:326
  48.8 12.3 %join.1 = (f32[64,512]{1,0:T(8,128)}, f32[3,64,512]{2,1,0:T(8,128)}, s32[64,128]{1,0:T(8,128)}) custom-call(bf16[9728,128]{1,0:T(8,128)(2,1)S(1)} %bitcast.7), custom_call_target="tpu_custom_call" | custom-call | tf_op jit(solution)/shard_map/join/pallas_call | solution.py:301

commit v6 on v5

--- a/solution.py
+++ b/solution.py
@@ -18,7 +18,7 @@
 GAP = 20
 HIGH = 8
 LOW = 64
-STRIDE = 72
+STRIDE = 40
 META = 256
 SOURCES = 32
 TALLY = DEVICES * LISTS // 128
@@ -26,6 +26,7 @@
 F32 = jnp.float32
 BF16 = jnp.bfloat16
 I32 = jnp.int32
+F8 = jnp.float8_e4m3fn
 VMEM = pl.BlockSpec(memory_space=pltpu.VMEM)
 NT = (((1,), (1,)), ((), ()))
 
@@ -214,7 +215,7 @@
                 jnp.concatenate([jnp.where(low == tally_ids[j], one, zero) for j in range(8)], 0)
             )
         a = jnp.concatenate(a_parts, axis=1)
-        b = jnp.concatenate(b_parts, axis=1)
+        b = jnp.concatenate(b_parts, axis=1).astype(F8)
         return sums + lax.dot_general(a, b, NT, preferred_element_type=F32)
 
     sums = lax.fori_loop(0, TALLY // GROUP, tally, jnp.zeros((64, 128), F32))
@@ -222,9 +223,7 @@
     copy.wait()
 
     low_id = iota((LOW, 128), 0).astype(F32).astype(BF16)
-    high_id = [
-        ((iota((16, 128), 0) >> 3) + (2 * j - 4)).astype(F32).astype(BF16) for j in range(HIGH // 2)
-    ]
+    high_id = ((iota((16, 128), 0) & 7) - 4).astype(F32).astype(BF16)
 
     def body(i, carry):
         for pair in range(SOURCES // 2):
@@ -235,24 +234,35 @@
                 a_parts, b_parts = [], []
                 for half in range(2):
                     at = src * ROWS + (2 * k + half) * VALUES
-                    index = jnp.broadcast_to(work[at : at + 1, :], (8, 128))
+                    index = twice(jnp.broadcast_to(work[at : at + 1, :], (8, 128)))
                     high = jnp.floor(index * (1.0 / LOW))
-                    low = twice(index - high * LOW)
-                    high = twice(high)
+                    low = index - high * LOW
                     low_all = jnp.concatenate([low] * (LOW // 16), axis=0)
                     b_parts.append(jnp.where(low_all == low_id, one, zero))
-                    group = twice(work[at : at + 8, :])
+                    here = high == high_id
+                    wide = [
+                        jnp.broadcast_to(work[at + c : at + c + 1, :], (8, 128))
+                        for c in range(1, VALUES)
+                    ]
+                    wide.append(wide[-1])
                     a_parts.append(
                         jnp.concatenate(
-                            [jnp.where(high == high_id[j], group, zero) for j in range(HIGH // 2)],
+                            [
+                                jnp.where(
+                                    here,
+                                    jnp.concatenate(wide[c : c + 2], axis=0).astype(BF16),
+                                    zero,
+                                )
+                                for c in range(0, VALUES, 2)
+                            ],
                             axis=0,
                         )
                     )
                 a = jnp.concatenate(a_parts, axis=1)
-                b = jnp.concatenate(b_parts, axis=1)
+                b = jnp.concatenate(b_parts, axis=1).astype(F8)
                 part = lax.dot_general(a, b, NT, preferred_element_type=F32)
                 at = pl.multiple_of(heads_smem[k, i * (SOURCES // 2) + src // 2 + src % 2 * (DEVICES // 2)], 8)
-                total[pl.ds(at, HIGH * 8), 0:LOW] += part
+                total[pl.ds(at, STRIDE), 0:LOW] += part[0:STRIDE]
         return carry
 
     lax.fori_loop(0, DEVICES // SOURCES, body, 0)
@@ -260,7 +270,7 @@
     for h in range(HIGH):
 
         def channel(c):
-            return total[pl.ds(h * 8 + c, BLOCKS, stride=STRIDE), :][:, 0:LOW]
+            return total[pl.ds((c - 1) * HIGH + h, BLOCKS, stride=STRIDE), :][:, 0:LOW]
 
         span = slice(h * LOW, (h + 1) * LOW)
         divisor = jnp.maximum(channel(1), 1.0)

time: 61.2 us -> 59.6 us (0.974)
  Pallas kernels: 15.2 us -> 13.6 us
    pallas_call x1, Pallas kernels: 12.3 us -> 10.7 us  [join(): pl.pallas_call(join_kernel, out_shape=(jax.ShapeDtypeStruct((BLOCKS, 512)...]
where the time goes in v6:
time: 59.6 us; the launch traced here: 59.5 us
  blocking collectives  45.2 us (76%)
  Pallas kernels  13.6 us (23%)
  between operations  0.64 us (1%)
    all_to_all x1, blocking collectives, on_device(): got = lax.all_to_all(send, AXES, split_axis=0, concat_axis=0, tiled=True)  45.2 us
    pallas_call x1, Pallas kernels, join(): pl.pallas_call(join_kernel, out_shape=(jax.ShapeDtypeStruct((BLOCKS, 512)...  10.7 us
    pallas_call x1, Pallas kernels, pack(): pl.pallas_call(pack_kernel, out_shape=jax.ShapeDtypeStruct((DEVICES * ROW...  2.87 us

profile of v6, /device:TPU:1, one launch (start us, length us, event | category | flops | bytes accessed | tf_op | source)
XLA Modules:
  0.0 59.5 jit_solution(17372386807150390399)
XLA Ops:
  0.6 2.9 %pack.1 = bf16[9728,128]{1,0:T(8,128)(2,1)S(1)} custom-call(s32[1,192]{1,0:T(1,128)} %bitcast.10, s32[64,128]{1,0:T(8,128)} %bitcast.9, s32[1,192]{1,0:T(1,128)} %bitcast.11, s32[192,256]{1,0:T(8,128)} %refs_3_.1, s32[192,256]{1,0:T(8,128)} %refs_4_.1, f32[192,256]{1,0:T(8,128)} %refs_5_.1, f32[192,256]{1,0:T(8,128)} %refs_6_.1, f32[3,192,256]{2,1,0:T(8,128)} %refs_7_.1), custom_call_target="tpu_custom_call" | custom-call | tf_op jit(solution)/shard_map/pack/pallas_call | solution.py:293
  3.5 45.2 %all_to_all.5 = bf16[128,38,2,128]{3,2,1,0:T(2,128)(2,1)S(1)} all-to-all(bf16[128,38,2,128]{3,2,1,0:T(2,128)(2,1)S(1)} %bitcast.8), channel_id=1, replica_groups=mesh['view'=8,'tile'=16] {'view','tile'}, dimensions={0} | all-to-all | bytes 4980736 | tf_op jit(solution)/shard_map/all_to_all | solution.py:336
  48.8 10.7 %join.1 = (f32[64,512]{1,0:T(8,128)}, f32[3,64,512]{2,1,0:T(8,128)}, s32[64,128]{1,0:T(8,128)}) custom-call(bf16[9728,128]{1,0:T(8,128)(2,1)S(1)} %bitcast.7), custom_call_target="tpu_custom_call" | custom-call | tf_op jit(solution)/shard_map/join/pallas_call | solution.py:311

commit v7 on v6

--- a/solution.py
+++ b/solution.py
@@ -15,6 +15,7 @@
 DATA = CAP * VALUES * 2
 ROWS = DATA + 4
 PAIR = 2 * ROWS
+SIDE = DEVICES // 2
 GAP = 20
 HIGH = 8
 LOW = 64
@@ -44,8 +45,8 @@
 
 
 def pack_kernel(*refs):
-    given, send, x, rows, place = refs[:8], refs[8], refs[9], refs[10], refs[11]
-    held, sems = refs[12:20], refs[20]
+    given, send, x, place, rows = refs[:8], refs[8], refs[9], refs[10], refs[11:13]
+    held, sems = refs[13:21], refs[21]
     copies = [
         pltpu.make_async_copy(src, dst, sems.at[i]) for i, (src, dst) in enumerate(zip(given, held))
     ]
@@ -66,10 +67,12 @@
     owner_hot = jnp.where(owner.astype(I32) == iota((DEVICES, LISTS), 0), 1.0, 0.0)
     before = hot(iota((LISTS, LISTS), 0) < iota((LISTS, LISTS), 1))
     order = jnp.sum(dot(owner_hot.astype(BF16), before) * owner_hot, axis=0, keepdims=True)
-    for k in range(CAP):
-        place[k * DEVICES : (k + 1) * DEVICES, :] = jnp.where(order == k, owner_hot, 0.0).astype(
-            BF16
-        )
+    for side in range(2):
+        for k in range(CAP):
+            at = (side * CAP + k) * SIDE
+            place[at : at + SIDE, :] = jnp.where(
+                order == k, owner_hot[side * SIDE : (side + 1) * SIDE], 0.0
+            ).astype(BF16)
 
     copies[2].wait()
     copies[3].wait()
@@ -102,11 +105,9 @@
         ]
     head = jnp.concatenate(lines, axis=0)
 
-    def spread_head(i, carry):
-        rows[pl.ds(i * ROWS + DATA, 4), :] = head
-        return carry
-
-    lax.fori_loop(0, DEVICES, spread_head, 0, unroll=8)
+    for i in range(SIDE):
+        for side in range(2):
+            rows[side][i * ROWS + DATA : (i + 1) * ROWS, :] = head
 
     for copy in copies[4:]:
         copy.wait()
@@ -125,19 +126,29 @@
             j = half * VALUES + v
             x[:, j * 128 : (j + 1) * 128] = value[:, half * 128 : (half + 1) * 128]
 
+    def move(side, j):
+        span = slice(side * CAP * SIDE, (side + 1) * CAP * SIDE)
+        moved = dot(place[span, :], x[:, j * 128 : (j + 2) * 128])
+        for k in range(CAP):
+            for part in range(2):
+                at = k * 2 * VALUES + j + part
+                rows[side][pl.ds(at, SIDE, stride=ROWS), :] = moved[
+                    k * SIDE : (k + 1) * SIDE, part * 128 : (part + 1) * 128
+                ]
+
+    def convert(side, pair):
+        at = pair * PAIR
+        to = side * SIDE * ROWS + at
+        send[to : to + PAIR, :] = rows[side][at : at + PAIR, :].astype(BF16)
+
     for j in range(0, 2 * VALUES, 2):
-        for k in range(CAP):
-            moved = dot(place[k * DEVICES : (k + 1) * DEVICES, :], x[:, j * 128 : (j + 2) * 128])
-            for side in range(2):
-                at = k * 2 * VALUES + j + side
-                rows[pl.ds(at, DEVICES, stride=ROWS), :] = moved[:, side * 128 : (side + 1) * 128]
-
-    def convert(i, carry):
-        at = pl.multiple_of(i * PAIR, PAIR)
-        send[pl.ds(at, PAIR), :] = rows[pl.ds(at, PAIR), :].astype(BF16)
-        return carry
-
-    lax.fori_loop(0, DEVICES // 2, convert, 0, unroll=4)
+        move(0, j)
+    for j in range(0, 2 * VALUES, 2):
+        move(1, j)
+        for pair in range(j * SIDE // 24, (j + 2) * SIDE // 24):
+            convert(0, pair)
+    for pair in range(SIDE // 2):
+        convert(1, pair)
 
 
 def twice(rows8):
@@ -148,7 +159,10 @@
     return [(iota((16, 128), 0) + 16 * j).astype(F32).astype(BF16) for j in range(count)]
 
 
-def join_kernel(got, tsdf, color, counts, total, work, info, lines, heads, heads_smem, sem):
+def join_kernel(
+    got, tsdf, color, counts, total, work, info, lines, heads, heads_smem, sem, tsdf_now, color_now,
+    counts_now, out_sems
+):
     me = lax.axis_index("view") * 16 + lax.axis_index("tile")
     one, zero = jnp.ones((), BF16), jnp.zeros((), BF16)
 
@@ -219,7 +233,9 @@
         return sums + lax.dot_general(a, b, NT, preferred_element_type=F32)
 
     sums = lax.fori_loop(0, TALLY // GROUP, tally, jnp.zeros((64, 128), F32))
-    counts[...] = sums.astype(I32)
+    counts_now[...] = sums.astype(I32)
+    copies = [pltpu.make_async_copy(counts_now, counts, out_sems.at[0])]
+    copies[0].start()
     copy.wait()
 
     low_id = iota((LOW, 128), 0).astype(F32).astype(BF16)
@@ -272,11 +288,26 @@
         def channel(c):
             return total[pl.ds((c - 1) * HIGH + h, BLOCKS, stride=STRIDE), :][:, 0:LOW]
 
-        span = slice(h * LOW, (h + 1) * LOW)
+        part = h // (HIGH // 2)
+        at = h % (HIGH // 2) * LOW
         divisor = jnp.maximum(channel(1), 1.0)
-        tsdf[:, span] = channel(2) / divisor
+        tsdf_now[part, :, at : at + LOW] = channel(2) / divisor
         for c in range(3):
-            color[c, :, span] = channel(3 + c) / divisor
+            color_now[part, c, :, at : at + LOW] = channel(3 + c) / divisor
+        if h % (HIGH // 2) == HIGH // 2 - 1:
+            half = pl.ds(part * 256, 256)
+            copies += [
+                pltpu.make_async_copy(
+                    tsdf_now.at[part], tsdf.at[:, half], out_sems.at[1 + 2 * part]
+                ),
+                pltpu.make_async_copy(
+                    color_now.at[part], color.at[:, :, half], out_sems.at[2 + 2 * part]
+                ),
+            ]
+            copies[-2].start()
+            copies[-1].start()
+    for copy in copies:
+        copy.wait()
 
 
 def pack(sdf_value, weight, color, voxel_index, valid, list_count, list_key, owner_slot):
@@ -297,8 +328,9 @@
         out_specs=VMEM,
         scratch_shapes=[
             pltpu.VMEM((LISTS, 2 * VALUES * 128), BF16),
-            pltpu.VMEM((DEVICES * ROWS, 128), F32),
             pltpu.VMEM((CAP * DEVICES, LISTS), BF16),
+            pltpu.VMEM((SIDE * ROWS, 128), F32),
+            pltpu.VMEM((SIDE * ROWS, 128), F32),
             *(pltpu.VMEM(array.shape, array.dtype) for array in given),
             pltpu.SemaphoreType.DMA((8,)),
         ],
@@ -316,7 +348,7 @@
             jax.ShapeDtypeStruct((64, 128), I32),
         ),
         in_specs=[VMEM],
-        out_specs=(VMEM, VMEM, VMEM),
+        out_specs=[pl.BlockSpec(memory_space=pl.ANY)] * 3,
         scratch_shapes=[
             pltpu.VMEM(((BLOCKS + 1) * STRIDE, 128), F32),
             pltpu.VMEM((SOURCES * ROWS, 128), F32),
@@ -325,6 +357,10 @@
             pltpu.VMEM((8, DEVICES), I32),
             pltpu.SMEM((8, DEVICES), I32),
             pltpu.SemaphoreType.DMA,
+            pltpu.VMEM((2, BLOCKS, 256), F32),
+            pltpu.VMEM((2, 3, BLOCKS, 256), F32),
+            pltpu.VMEM((64, 128), I32),
+            pltpu.SemaphoreType.DMA((5,)),
         ],
         compiler_params=pltpu.CompilerParams(vmem_limit_bytes=20 * 2**20),
         name="join",

time: 59.6 us -> 59.4 us (level)
  no operation moved by 1% of the time
where the time goes in v7:
time: 59.4 us; the launch traced here: 59.2 us
  blocking collectives  45.2 us (76%)
  Pallas kernels  13.4 us (23%)
  between operations  0.64 us (1%)
    all_to_all x1, blocking collectives, on_device(): got = lax.all_to_all(send, AXES, split_axis=0, concat_axis=0, tiled=True)  45.2 us
    pallas_call x1, Pallas kernels, join(): pl.pallas_call(join_kernel, out_shape=(jax.ShapeDtypeStruct((BLOCKS, 512)...  10.6 us
    pallas_call x1, Pallas kernels, pack(): pl.pallas_call(pack_kernel, out_shape=jax.ShapeDtypeStruct((DEVICES * ROW...  2.72 us

profile of v7, /device:TPU:1, one launch (start us, length us, event | category | flops | bytes accessed | tf_op | source)
XLA Modules:
  0.0 59.2 jit_solution(4234265170873964070)
XLA Ops:
  0.6 2.7 %pack.1 = bf16[9728,128]{1,0:T(8,128)(2,1)S(1)} custom-call(s32[1,192]{1,0:T(1,128)} %bitcast.10, s32[64,128]{1,0:T(8,128)} %bitcast.9, s32[1,192]{1,0:T(1,128)} %bitcast.11, s32[192,256]{1,0:T(8,128)} %refs_3_.1, s32[192,256]{1,0:T(8,128)} %refs_4_.1, f32[192,256]{1,0:T(8,128)} %refs_5_.1, f32[192,256]{1,0:T(8,128)} %refs_6_.1, f32[3,192,256]{2,1,0:T(8,128)} %refs_7_.1), custom_call_target="tpu_custom_call" | custom-call | tf_op jit(solution)/shard_map/pack/pallas_call | solution.py:324
  3.4 45.2 %all_to_all.5 = bf16[128,38,2,128]{3,2,1,0:T(2,128)(2,1)S(1)} all-to-all(bf16[128,38,2,128]{3,2,1,0:T(2,128)(2,1)S(1)} %bitcast.8), channel_id=1, replica_groups=mesh['view'=8,'tile'=16] {'view','tile'}, dimensions={0} | all-to-all | bytes 4980736 | tf_op jit(solution)/shard_map/all_to_all | solution.py:372
  48.6 10.6 %join.1 = (f32[64,512]{1,0:T(8,128)}, f32[3,64,512]{2,1,0:T(8,128)}, s32[64,128]{1,0:T(8,128)}) custom-call(bf16[9728,128]{1,0:T(8,128)(2,1)S(1)} %bitcast.7), custom_call_target="tpu_custom_call" | custom-call | tf_op jit(solution)/shard_map/join/pallas_call | solution.py:343

commit v8 on v7

--- a/solution.py
+++ b/solution.py
@@ -159,10 +159,7 @@
     return [(iota((16, 128), 0) + 16 * j).astype(F32).astype(BF16) for j in range(count)]
 
 
-def join_kernel(
-    got, tsdf, color, counts, total, work, info, lines, heads, heads_smem, sem, tsdf_now, color_now,
-    counts_now, out_sems
-):
+def join_kernel(got, tsdf, color, counts, total, work, info, lines, heads, heads_smem, sem):
     me = lax.axis_index("view") * 16 + lax.axis_index("tile")
     one, zero = jnp.ones((), BF16), jnp.zeros((), BF16)
 
@@ -203,8 +200,6 @@
     found = found.astype(I32)
     heads[...] = jnp.where(found == 0, BLOCKS, found - 1) * STRIDE
     copy = pltpu.make_async_copy(heads, heads_smem, sem)
-    copy.start()
-
     total[...] = jnp.zeros_like(total)
 
     left = iota((DEVICES // 2, 128), 1) < 64
@@ -213,6 +208,7 @@
         lines[p, DEVICES:TALLY, :] = jnp.where(
             left, rest[p][0 : DEVICES // 2], rest[p][DEVICES // 2 : DEVICES]
         )
+    copy.start()
     tally_ids = ids(8)
 
     def tally(g, sums):
@@ -233,9 +229,7 @@
         return sums + lax.dot_general(a, b, NT, preferred_element_type=F32)
 
     sums = lax.fori_loop(0, TALLY // GROUP, tally, jnp.zeros((64, 128), F32))
-    counts_now[...] = sums.astype(I32)
-    copies = [pltpu.make_async_copy(counts_now, counts, out_sems.at[0])]
-    copies[0].start()
+    counts[...] = sums.astype(I32)
     copy.wait()
 
     low_id = iota((LOW, 128), 0).astype(F32).astype(BF16)
@@ -288,26 +282,11 @@
         def channel(c):
             return total[pl.ds((c - 1) * HIGH + h, BLOCKS, stride=STRIDE), :][:, 0:LOW]
 
-        part = h // (HIGH // 2)
-        at = h % (HIGH // 2) * LOW
+        span = slice(h * LOW, (h + 1) * LOW)
         divisor = jnp.maximum(channel(1), 1.0)
-        tsdf_now[part, :, at : at + LOW] = channel(2) / divisor
+        tsdf[:, span] = channel(2) / divisor
         for c in range(3):
-            color_now[part, c, :, at : at + LOW] = channel(3 + c) / divisor
-        if h % (HIGH // 2) == HIGH // 2 - 1:
-            half = pl.ds(part * 256, 256)
-            copies += [
-                pltpu.make_async_copy(
-                    tsdf_now.at[part], tsdf.at[:, half], out_sems.at[1 + 2 * part]
-                ),
-                pltpu.make_async_copy(
-                    color_now.at[part], color.at[:, :, half], out_sems.at[2 + 2 * part]
-                ),
-            ]
-            copies[-2].start()
-            copies[-1].start()
-    for copy in copies:
-        copy.wait()
+            color[c, :, span] = channel(3 + c) / divisor
 
 
 def pack(sdf_value, weight, color, voxel_index, valid, list_count, list_key, owner_slot):
@@ -348,7 +327,7 @@
             jax.ShapeDtypeStruct((64, 128), I32),
         ),
         in_specs=[VMEM],
-        out_specs=[pl.BlockSpec(memory_space=pl.ANY)] * 3,
+        out_specs=(VMEM, VMEM, VMEM),
         scratch_shapes=[
             pltpu.VMEM(((BLOCKS + 1) * STRIDE, 128), F32),
             pltpu.VMEM((SOURCES * ROWS, 128), F32),
@@ -357,10 +336,6 @@
             pltpu.VMEM((8, DEVICES), I32),
             pltpu.SMEM((8, DEVICES), I32),
             pltpu.SemaphoreType.DMA,
-            pltpu.VMEM((2, BLOCKS, 256), F32),
-            pltpu.VMEM((2, 3, BLOCKS, 256), F32),
-            pltpu.VMEM((64, 128), I32),
-            pltpu.SemaphoreType.DMA((5,)),
         ],
         compiler_params=pltpu.CompilerParams(vmem_limit_bytes=20 * 2**20),
         name="join",

time: 59.4 us -> 59.4 us (level)
  no operation moved by 1% of the time
where the time goes in v8:
time: 59.4 us; the launch traced here: 59.3 us
  blocking collectives  45.2 us (76%)
  Pallas kernels  13.4 us (23%)
  between operations  0.64 us (1%)
    all_to_all x1, blocking collectives, on_device(): got = lax.all_to_all(send, AXES, split_axis=0, concat_axis=0, tiled=True)  45.2 us
    pallas_call x1, Pallas kernels, join(): pl.pallas_call(join_kernel, out_shape=(jax.ShapeDtypeStruct((BLOCKS, 512)...  10.7 us
    pallas_call x1, Pallas kernels, pack(): pl.pallas_call(pack_kernel, out_shape=jax.ShapeDtypeStruct((DEVICES * ROW...  2.72 us

profile of v8, /device:TPU:1, one launch (start us, length us, event | category | flops | bytes accessed | tf_op | source)
XLA Modules:
  0.0 59.3 jit_solution(11879950437172202703)
XLA Ops:
  0.6 2.7 %pack.1 = bf16[9728,128]{1,0:T(8,128)(2,1)S(1)} custom-call(s32[1,192]{1,0:T(1,128)} %bitcast.10, s32[64,128]{1,0:T(8,128)} %bitcast.9, s32[1,192]{1,0:T(1,128)} %bitcast.11, s32[192,256]{1,0:T(8,128)} %refs_3_.1, s32[192,256]{1,0:T(8,128)} %refs_4_.1, f32[192,256]{1,0:T(8,128)} %refs_5_.1, f32[192,256]{1,0:T(8,128)} %refs_6_.1, f32[3,192,256]{2,1,0:T(8,128)} %refs_7_.1), custom_call_target="tpu_custom_call" | custom-call | tf_op jit(solution)/shard_map/pack/pallas_call | solution.py:303
  3.4 45.2 %all_to_all.5 = bf16[128,38,2,128]{3,2,1,0:T(2,128)(2,1)S(1)} all-to-all(bf16[128,38,2,128]{3,2,1,0:T(2,128)(2,1)S(1)} %bitcast.8), channel_id=1, replica_groups=mesh['view'=8,'tile'=16] {'view','tile'}, dimensions={0} | all-to-all | bytes 4980736 | tf_op jit(solution)/shard_map/all_to_all | solution.py:347
  48.6 10.7 %join.1 = (f32[64,512]{1,0:T(8,128)}, f32[3,64,512]{2,1,0:T(8,128)}, s32[64,128]{1,0:T(8,128)}) custom-call(bf16[9728,128]{1,0:T(8,128)(2,1)S(1)} %bitcast.7), custom_call_target="tpu_custom_call" | custom-call | tf_op jit(solution)/shard_map/join/pallas_call | solution.py:322
